TPU v7x, 32 devices: a whole 2x2x4 slice. The times are simulated.
32 devices in a mesh: row: 4 (over y, core), col: 8 (over z, x).
Axes of the slice: x: 2, y: 2, z: 4, core: 2. Of those that a mesh axis runs over, the one named last changes fastest.
Arguments:
- values: bfloat16 [8192, 128], P('row'), may hold values from -30 to 30
- points0: bfloat16 [2, 8192], P(None, 'row'), may hold values from 0 to 1
- points1: bfloat16 [2, 2048], P(None, 'row'), may hold values from 0 to 1
- points2: bfloat16 [2, 256], P(None, 'row'), may hold values from 0 to 1
- tiles_a0: int32 [4, 8, 2, 48], P('row', 'col'), may hold values from 0 to 15, as said below
- tiles_e1: int32 [4, 8, 2, 20], P('row', 'col'), may hold values from 0 to 15, as said below
- tiles_a1: int32 [4, 8, 2, 4], P('row', 'col'), may hold values from 0 to 3, as said below
- factor: bfloat16 [256, 256], P('row', 'col'), as said below
Outputs:
- fine_coef: float32 [8192, 128], P(('row', 'col'))
- mid_coef: float32 [2048, 128], P('col')
- coarse_coef: float32 [256, 128], P('row')
- norms: float32 [1], replicated
Inputs may be any that keep to these rules, and one draw needn't show every extreme that they name: `tiles_a0`: within each block the 48 listed tile pairs are distinct; tile rows are below 16 and tile columns below 8. `tiles_e1`: within each block the 20 listed tile pairs are distinct; tile rows are below 16 and tile columns below 2. `tiles_a1`: within each block the 4 listed tile pairs are distinct; tile rows are below 4 and tile columns below 2. `factor`: upper triangular; diagonal entries from 1 to 2.
All inputs are finite; a program needn't handle non-finite values.
Results may differ from a plain program's by a relative error of at most 0.0042.
Values may be sent and summed in bfloat16 or wider, within the bound.
A program may use at most 64 MiB of HBM per device.

v0:
```python
import functools
import math

import jax
import jax.numpy as jnp
from jax import lax
from jax.experimental import pallas as pl
from jax.experimental.pallas import tpu as pltpu
from jax.sharding import PartitionSpec as P

TILE = 128


support_fine = 0.35
support_mid = 0.55
support_coarse = 0.8


def spread(x, axis, root):
    mine = lax.axis_index(axis) == root
    return lax.psum(jnp.where(mine, x, jnp.zeros_like(x)), axis)


def wendland(left_pts, right_pts, support):
    left = left_pts.astype(jnp.float32)
    right = right_pts.astype(jnp.float32)
    across = left[0][..., :, None] - right[0][..., None, :]
    upward = left[1][..., :, None] - right[1][..., None, :]
    ratio_t = jnp.sqrt(across * across + upward * upward) / support
    margin = jnp.maximum(1.0 - ratio_t, 0.0)
    squared = margin * margin
    return (squared * squared * (4.0 * ratio_t + 1.0)).astype(jnp.bfloat16)


def listed_terms(row_pts, col_pts, listing, vector, support, flipped):
    row_tiles = row_pts.reshape(2, -1, TILE)
    col_tiles = col_pts.reshape(2, -1, TILE)
    listed = listing.shape[-1]
    group = math.gcd(listed, 32)
    order = listing.reshape(2, listed // group, group)
    fields = vector.shape[-1]
    inputs = vector.reshape(-1, TILE, fields)
    target = col_tiles.shape[1] if flipped else row_tiles.shape[1]
    total = jnp.zeros((target, TILE, fields), jnp.float32)

    def add_group(total, pair):
        tile_rows, tile_cols = pair
        kernel = wendland(row_tiles[:, tile_rows], col_tiles[:, tile_cols], support)
        if flipped:
            contrib = jnp.einsum(
                "gij,gir->gjr", kernel, inputs[tile_rows], preferred_element_type=jnp.float32
            )
            return (total.at[tile_cols].add(contrib), None)
        contrib = jnp.einsum(
            "gij,gjr->gir", kernel, inputs[tile_cols], preferred_element_type=jnp.float32
        )
        return (total.at[tile_rows].add(contrib), None)

    total, unused = lax.scan(add_group, total, (order[0], order[1]))
    return total.reshape(-1, fields)


def per_device(values, points0, points1, points2, tiles_a0, tiles_e1, tiles_a1, factor):
    row_count = lax.axis_size("row")
    col_count = lax.axis_size("col")
    col_id = lax.axis_index("col")
    col_per_row = col_count // row_count
    rows_fine, fields = values.shape
    rows_mid = points1.shape[1]
    share = rows_fine // col_count
    cols_fine = rows_fine // col_per_row
    cols_mid = rows_mid // col_per_row
    source = col_id // col_per_row
    part_index = col_id % col_per_row
    value_piece = lax.dynamic_slice_in_dim(values, part_index * cols_fine, cols_fine, 0)
    fine_piece = lax.dynamic_slice_in_dim(points0, part_index * cols_fine, cols_fine, 1)
    mid_piece = lax.dynamic_slice_in_dim(points1, part_index * cols_mid, cols_mid, 1)
    value_cols, fine_cols, mid_cols = (
        spread(value_piece, "row", source),
        spread(fine_piece, "row", source),
        spread(mid_piece, "row", source),
    )
    scale_a0 = (rows_fine / (col_count * tiles_a0.shape[-1] * TILE * TILE)) ** 0.5
    scale_e1 = (rows_fine / (col_count * tiles_e1.shape[-1] * TILE * TILE)) ** 0.5
    scale_a1 = (rows_mid / (col_count * tiles_a1.shape[-1] * TILE * TILE)) ** 0.5
    scale_e2 = (1.0 / (rows_mid * row_count)) ** 0.5
    fine_data = values.astype(jnp.float32)
    own_data = lax.dynamic_slice_in_dim(values, col_id * share, share, 0).astype(jnp.float32)
    product_part = listed_terms(points0, fine_cols, tiles_a0[0, 0], value_cols, support_fine, False)
    product_whole = lax.psum(product_part, "col")
    fine_residual = fine_data - 0.5 * (scale_a0 * product_whole)
    fine_square = jnp.sum(fine_residual * fine_residual)
    restrict_part = listed_terms(
        points0, mid_cols, tiles_e1[0, 0], fine_residual.astype(jnp.bfloat16), support_mid, True
    )
    restrict_sum = lax.psum(restrict_part, "row")
    mid_data = scale_e1 * restrict_sum
    mid_part = listed_terms(
        points1, mid_cols, tiles_a1[0, 0], mid_data.astype(jnp.bfloat16), support_mid, False
    )
    mid_whole = (scale_a1 * lax.psum(mid_part, "col")).astype(jnp.bfloat16)
    mid_slice = lax.dynamic_slice_in_dim(mid_whole, part_index * cols_mid, cols_mid, 0)
    mid_turned = spread(mid_slice, "row", source)
    mid_residual = mid_data - 0.5 * mid_turned.astype(jnp.float32)
    coarse_kernel = wendland(points2, mid_cols, support_coarse)
    coarse_part = jnp.dot(
        coarse_kernel, mid_residual.astype(jnp.bfloat16), preferred_element_type=jnp.float32
    )
    coarse_sum = lax.psum(coarse_part, "col")
    coarse_data = (scale_e2 * coarse_sum).astype(jnp.bfloat16)
    halfway_part = lax.dot_general(
        factor, coarse_data, (((0,), (0,)), ((), ())), preferred_element_type=jnp.float32
    )
    halfway = lax.psum(halfway_part, "row").astype(jnp.bfloat16)
    coarse_part_two = jnp.dot(factor, halfway, preferred_element_type=jnp.float32)
    coarse_coef = lax.psum(coarse_part_two, "col")
    prolong_part = lax.dot_general(
        coarse_kernel,
        coarse_coef.astype(jnp.bfloat16),
        (((0,), (0,)), ((), ())),
        preferred_element_type=jnp.float32,
    )
    mid_coef = 0.5 * mid_data + scale_e2 * lax.psum(prolong_part, "row")
    fine_part = listed_terms(
        points0, mid_cols, tiles_e1[0, 0], mid_coef.astype(jnp.bfloat16), support_mid, False
    )
    fine_coef = 0.5 * own_data + scale_e1 * lax.psum_scatter(
        fine_part, "col", scatter_dimension=0, tiled=True
    )
    fine_total = lax.psum(fine_square / col_count, ("row", "col"))
    fine_norm = fine_total / (rows_fine * row_count * fields)
    return (fine_coef, mid_coef, coarse_coef, jnp.stack([fine_norm]))


FAR = 1024.0
CHUNKS = 4
MESH = pl.DeviceIdType.MESH


def phi_tile(cx, cy, rx, ry, inv_square):
    across = cx - rx
    upward = cy - ry
    square = (across * across + upward * upward) * inv_square
    t = square * lax.rsqrt(jnp.maximum(square, 1e-30))
    margin = jnp.maximum(1.0 - t, 0.0)
    squared = margin * margin
    return (squared * squared * (4.0 * t + 1.0)).astype(jnp.bfloat16)


def dot(a, b):
    return jnp.dot(a, b, preferred_element_type=jnp.float32)


def far_rows(tiles, row_tiles, col_tiles, by_col):
    row, col = tiles[0, 0, 0:1, :], tiles[0, 0, 1:2, :]
    key = col * row_tiles + row if by_col else row * col_tiles + col
    count = row_tiles * col_tiles
    place = lax.broadcasted_iota(jnp.int32, (count, key.shape[1]), 0)
    near = jnp.max(jnp.where(place == key, 1.0, 0.0), axis=1, keepdims=True)
    return jnp.broadcast_to(FAR * (1.0 - near), (count, TILE))


def cycle_kernel(g, vals, points0, points1, points2, tiles_a0, tiles_e1, tiles_a1, factor, fine_o, mid_o, coarse_o, norm_o,
                 pts, offs, fac, offe, offa, ptsg, offg, facg, vall, a0, e1own, e1t, e2t, e2c, a1, cf, cm, cc2, resg, part_buf,
                 rsin, midc, mida, rhs, csend, crecv, cg, gall, gt, ccoef, mcb,
                 p_s, p_r, o_s, o_r, f_s, f_r, vy_s, vy_r, vx_s, vx_r, vf_s, vf_r, vg_s, vg_r, vp_s, vp_r,
                 g_s, g_r, res_s, res_r, rs_s, rs_r, mc_s, mc_r, mq_s, mq_r, mf_s, mf_r, cr_s, cr_r, ca_s, ca_r):
    nr, nc, R0, R1, R2 = g["nr"], g["nc"], g["R0"], g["R1"], g["R2"]
    D = nr * nc
    T0, T1 = R0 // TILE, R1 // TILE
    C0, C1 = R0 * nr // nc, R1 * nr // nc
    B0, B1 = C0 // TILE, C1 // TILE
    S0 = R0 // nc
    I0 = S0 // TILE
    Q1 = C1 // nr
    CR = R2 * nr // D
    NT1 = nr * T1
    NT2 = nr * R2 // TILE
    X1, Y1, X2 = 2 * T0, 2 * T0 + T1, 2 * T0 + 2 * T1
    fine_inv, mid_inv, coarse_inv = (1.0 / (s * s) for s in (support_fine, support_mid, support_coarse))
    r = lax.axis_index("row")
    c = lax.axis_index("col")
    d = r * nc + c
    mate = r + 1 - 2 * lax.rem(r, 2)
    yp = lax.rem(r + 2, nr)
    diag = lax.rem(mate + 2, nr)
    h = lax.rem(c, 2)
    xp = c + 1 - 2 * h

    def rc(src, dst, ssem, rsem, rr, cc):
        return pltpu.make_async_remote_copy(src_ref=src, dst_ref=dst, send_sem=ssem, recv_sem=rsem,
                                            device_id=(rr, cc), device_id_type=MESH)

    def each(lo, hi, f):
        def body(k, carry):
            f(k)
            return carry
        lax.fori_loop(lo, hi, body, 0)

    barrier = pltpu.get_barrier_semaphore()

    def greet(k):
        peer = lax.rem(d + k, D)
        pl.semaphore_signal(barrier, inc=1, device_id=(peer // nc, lax.rem(peer, nc)), device_id_type=MESH)

    each(1, D, greet)
    pl.semaphore_wait(barrier, D - 1)

    pts[...] = jnp.zeros_like(pts)
    for way in range(2):
        for ref, at, count in ((points0, way * T0, T0), (points1, X1 + way * T1, T1)):
            line = ref[way:way + 1, :].astype(jnp.float32)
            for k in range(count):
                pts[at + k:at + k + 1, :] = line[:, k * TILE:(k + 1) * TILE]
        line = points2[way:way + 1, :].astype(jnp.float32)
        blank = jnp.zeros((1, TILE - R2), jnp.float32)
        pts[X2 + way:X2 + way + 1, :] = jnp.concatenate([line, blank], axis=1)
        pts[X2 + 2 + way:X2 + 3 + way, :] = jnp.concatenate([blank, line], axis=1)

    def row_send(src_of, dst, ss, rr):
        for k in range(1, nr):
            q = lax.rem(r + k, nr)
            rc(src_of(q), dst, ss.at[k], rr.at[r], q, c).start()

    def row_wait(src, dst_of, ss, rr):
        for k in range(1, nr):
            q = lax.rem(r + k, nr)
            rc(src, dst_of(q), ss.at[k], rr.at[q], q, c).wait()

    def col_send(src_of, dst, ss, rr):
        def go(k):
            q = lax.rem(c + k, nc)
            rc(src_of(q), dst, ss.at[k], rr.at[c], r, q).start()
        each(1, nc, go)

    def col_wait(src, dst_of, ss, rr):
        def go(k):
            q = lax.rem(c + k, nc)
            rc(src, dst_of(q), ss.at[k], rr.at[q], r, q).wait()
        each(1, nc, go)

    row_send(lambda q: pts, ptsg.at[r], p_s, p_r)
    HALF = R0 // 2
    CH = HALF // CHUNKS

    def chunk(half, q):
        return pl.ds(pl.multiple_of(half * HALF + q * CH, CH), CH)

    def y_copy(q):
        return rc(vals.at[chunk(h, q)], vall.at[r, chunk(h, q)], vy_s.at[q], vy_r.at[q], yp, c)

    def y_in(q):
        return rc(vals.at[chunk(h, q)], vall.at[yp, chunk(h, q)], vy_s.at[q], vy_r.at[q], yp, c)

    def x_copy(q):
        return rc(vall.at[yp, chunk(h, q)], vall.at[yp, chunk(h, q)], vx_s.at[q], vx_r.at[q], r, xp)

    def x_in(q):
        return rc(vall.at[yp, chunk(h, q)], vall.at[yp, chunk(1 - h, q)], vx_s.at[q], vx_r.at[q], r, xp)

    def f_copy(q):
        return rc(vall.at[yp, chunk(h, q)], vall.at[yp, chunk(h, q)], vf_s.at[q], vf_r.at[q], mate, c)

    def f_in(q):
        return rc(vall.at[yp, chunk(h, q)], vall.at[diag, chunk(h, q)], vf_s.at[q], vf_r.at[q], mate, c)

    def g_copy(q):
        return rc(vall.at[yp, chunk(1 - h, q)], vall.at[yp, chunk(1 - h, q)], vg_s.at[q], vg_r.at[q], mate, c)

    def g_in(q):
        return rc(vall.at[yp, chunk(1 - h, q)], vall.at[diag, chunk(1 - h, q)], vg_s.at[q], vg_r.at[q], mate, c)

    for q in range(CHUNKS):
        y_copy(q).start()
    mate_copy = rc(vals, vall.at[r], vp_s.at[0], vp_r.at[0], mate, c)
    mate_copy.start()
    far_a0 = far_rows(tiles_a0, T0, B0, False)
    far_e1 = far_rows(tiles_e1, T0, B1, False)
    offs[...] = jnp.zeros_like(offs)
    for q in range(nc):
        offs[q, :I0 * B0] = far_a0[q * I0 * B0:(q + 1) * I0 * B0]
        offs[q, I0 * B0:I0 * (B0 + B1)] = far_e1[q * I0 * B1:(q + 1) * I0 * B1]
    wide = factor.shape[1]
    lane_of = lax.rem(c, TILE // wide)
    raw = factor[...].astype(jnp.float32)
    fac[...] = jnp.concatenate([jnp.where(lane_of == k, raw, 0.0) for k in range(TILE // wide)], axis=1).astype(jnp.bfloat16)
    col_send(lambda q: offs.at[q], offg.at[c], o_s, o_r)
    col_send(lambda q: fac, facg.at[c], f_s, f_r)
    ptsg[r] = pts[...]
    offg[c] = offs[c]
    facg[c] = fac[...]

    offe[...] = far_rows(tiles_e1, T0, B1, True)
    offa[...] = far_rows(tiles_a1, T1, B1, False)

    def turned(row):
        return jnp.broadcast_to(row, (TILE, TILE)).T

    for i in range(I0):
        for way in range(2):
            cf[2 * i + way] = turned(pts[pl.ds(way * T0 + c * I0 + i, 1), :])
    row_wait(pts, lambda q: ptsg.at[q], p_s, p_r)
    col_wait(offs.at[0], lambda q: offg.at[q], o_s, o_r)

    blocks = (r, mate, yp, diag)
    for s, rb in enumerate(blocks):
        def build_a0(kk, s=s, rb=rb):
            rx = ptsg[rb, pl.ds(kk, 1), :]
            ry = ptsg[rb, pl.ds(T0 + kk, 1), :]
            cb = rb * (nc // nr) + kk // B0
            j = lax.rem(kk, B0)
            for i in range(I0):
                off = offg[cb, pl.ds(i * B0 + j, 1), :]
                a0[s, i * TILE:(i + 1) * TILE, pl.ds(pl.multiple_of(kk * TILE, TILE), TILE)] = phi_tile(
                    cf[2 * i], cf[2 * i + 1], rx + off, ry, fine_inv)
        each(0, T0, build_a0)
        if s < CHUNKS:
            y_in(s).wait_recv()
            x_copy(s).start()
            f_copy(s).start()
    acc = dot(a0[0], vals[...])
    for q in range(CHUNKS):
        x_in(q).wait_recv()
        g_copy(q).start()
    rc(vals, vall.at[mate], vp_s.at[0], vp_r.at[0], mate, c).wait_recv()
    acc = acc + dot(a0[1], vall[mate])
    acc = acc + dot(a0[2], vall[yp])
    for q in range(CHUNKS):
        f_in(q).wait_recv()
        g_in(q).wait_recv()
    acc = acc + dot(a0[3], vall[diag])
    own_vals = vals[pl.ds(pl.multiple_of(c * S0, S0), S0), :].astype(jnp.float32)
    res = own_vals - (0.5 * g["scale_a0"]) * acc

    def res_at(q):
        return resg.at[pl.ds(pl.multiple_of(q * S0, S0), S0)]

    resg[pl.ds(pl.multiple_of(c * S0, S0), S0), :] = res.astype(jnp.bfloat16)
    for k in range(1, nc // 2):
        q = lax.rem(c + 2 * k, nc)
        rc(res_at(c), res_at(c), res_s.at[k], res_r.at[c], r, q).start()
    rc(res_at(c), res_at(c), res_s.at[0], res_r.at[c], r, xp).start()

    def res_pass(k):
        q = lax.rem(c + 2 * k, nc)
        rc(res_at(c), res_at(q), res_s.at[k], res_r.at[q], r, q).wait_recv()
        rc(res_at(q), res_at(q), res_s.at[nc // 2 + k], res_r.at[q], r, xp).start()


    def turn_mid(k):
        for way in range(2):
            cm[k, way] = turned(ptsg[k // T1, pl.ds(X1 + way * T1 + lax.rem(k, T1), 1), :])
    each(0, NT1, turn_mid)
    res_pass(1)

    def build_e1t(i):
        rx, ry = pts[pl.ds(i, 1), :], pts[pl.ds(T0 + i, 1), :]
        for j in range(B1):
            off = offe[pl.ds(j * T0 + i, 1), :]
            e1t[j * TILE:(j + 1) * TILE, pl.ds(pl.multiple_of(i * TILE, TILE), TILE)] = phi_tile(
                cm[c * B1 + j, 0], cm[c * B1 + j, 1], rx + off, ry, mid_inv)
    each(0, T0, build_e1t)
    res_pass(nc // 2 - 1)
    for k in range(2, nc // 2 - 1):
        res_pass(k)
    col_wait(fac, lambda q: facg.at[q], f_s, f_r)
    per_lane = nc * TILE // g["N2"]
    for lane in range(g["N2"] // TILE):
        total = facg[lane * per_lane].astype(jnp.float32)
        for k in range(1, per_lane):
            total = total + facg[lane * per_lane + k].astype(jnp.float32)
        gall[r, :, lane * TILE:(lane + 1) * TILE] = total.astype(jnp.bfloat16)
    row_send(lambda q: gall.at[r], gall.at[r], g_s, g_r)

    def coarse_row(t, way):
        per = TILE // R2
        return ptsg[per * t, X2 + way:X2 + way + 1, :] + ptsg[per * t + 1, X2 + 2 + way:X2 + 3 + way, :]

    for i in range(T1):
        for j in range(B1):
            mt = c * B1 + j
            rx = ptsg[mt // T1, pl.ds(X1 + lax.rem(mt, T1), 1), :]
            ry = ptsg[mt // T1, pl.ds(Y1 + lax.rem(mt, T1), 1), :]
            off = offa[i * B1 + j:i * B1 + j + 1, :]
            a1[i * TILE:(i + 1) * TILE, j * TILE:(j + 1) * TILE] = phi_tile(
                cm[r * T1 + i, 0], cm[r * T1 + i, 1], rx + off, ry, mid_inv)
    for t in range(NT2):
        for way in range(2):
            cc2[2 * t + way] = turned(coarse_row(t, way))

    def build_e2c(k):
        mt = jnp.where(k < T1, r * T1 + k, c * B1 + k - T1)
        rx = ptsg[mt // T1, pl.ds(X1 + lax.rem(mt, T1), 1), :]
        ry = ptsg[mt // T1, pl.ds(Y1 + lax.rem(mt, T1), 1), :]
        for t in range(NT2):
            e2c[t * TILE:(t + 1) * TILE, pl.ds(pl.multiple_of(k * TILE, TILE), TILE)] = phi_tile(
                cc2[2 * t], cc2[2 * t + 1], rx, ry, coarse_inv)
    each(0, T1 + B1, build_e2c)

    for k in range(1, nc // 2):
        q = lax.rem(c + 2 * k, nc)
        rc(res_at(c), res_at(c), res_s.at[k], res_r.at[c], r, q).wait_send()
        rc(res_at(q), res_at(q), res_s.at[nc // 2 + k], res_r.at[q], r, xp).wait_send()
        qx = lax.rem(xp + 2 * k, nc)
        rc(res_at(qx), res_at(qx), res_s.at[0], res_r.at[qx], r, xp).wait_recv()
    rc(res_at(c), res_at(c), res_s.at[0], res_r.at[c], r, xp).wait_send()
    rc(res_at(c), res_at(xp), res_s.at[0], res_r.at[xp], r, xp).wait_recv()
    held = resg[...].astype(jnp.float32)
    square = jnp.sum((held * held).reshape(R0 // 8, 8, -1), axis=0)
    part_buf[...] = dot(e1t[...], resg[...]).reshape(nr, Q1, -1)
    row_send(lambda q: part_buf.at[q], rsin.at[r], rs_s, rs_r)
    rsin[r] = part_buf[r]
    row_wait(part_buf.at[0], lambda q: rsin.at[q], rs_s, rs_r)
    quarter = rsin[0]
    for k in range(1, nr):
        quarter = quarter + rsin[k]
    quarter = g["scale_e1"] * quarter
    midc[r] = jnp.concatenate([quarter, square], axis=0)
    mida[r, c] = quarter.astype(jnp.bfloat16)
    row_send(lambda q: midc.at[r], midc.at[r], mc_s, mc_r)
    col_send(lambda q: mida.at[r, c], mida.at[r, c], mq_s, mq_r)
    row_wait(midc.at[r], lambda q: midc.at[q], mc_s, mc_r)
    mid_f32 = midc[:, :Q1].reshape(C1, -1)
    mid_col = mid_f32.astype(jnp.bfloat16)
    rhs[:R1] = ((-0.5 * g["scale_a1"]) * dot(a1[...], mid_col)).astype(jnp.bfloat16)
    for k in range(nr):
        rhs[R1 + k * Q1:R1 + (k + 1) * Q1] = jnp.where(r == k, midc[k, :Q1], 0.0).astype(jnp.bfloat16)
    csend[...] = (g["scale_e2"] * dot(e2c[...], rhs[...])).reshape(D, CR, -1)

    def cr_go(k):
        peer = lax.rem(d + k, D)
        rc(csend.at[peer], crecv.at[d], cr_s.at[k], cr_r.at[d], peer // nc, lax.rem(peer, nc)).start()
    each(1, D, cr_go)
    crecv[d] = csend[d]
    def build_e1own(k):
        rx = ptsg[k // T1, pl.ds(X1 + lax.rem(k, T1), 1), :]
        ry = ptsg[k // T1, pl.ds(Y1 + lax.rem(k, T1), 1), :]
        for i in range(I0):
            off = offg[k // B1, pl.ds(I0 * B0 + i * B1 + lax.rem(k, B1), 1), :]
            e1own[i * TILE:(i + 1) * TILE, pl.ds(pl.multiple_of(k * TILE, TILE), TILE)] = phi_tile(
                cf[2 * i], cf[2 * i + 1], rx + off, ry, mid_inv)
    each(0, NT1, build_e1own)

    def build_e2t(k):
        for t in range(NT2):
            e2t[pl.ds(pl.multiple_of(k * TILE, TILE), TILE), t * TILE:(t + 1) * TILE] = phi_tile(
                cm[k, 0], cm[k, 1], coarse_row(t, 0), coarse_row(t, 1), coarse_inv)
    each(0, NT1, build_e2t)
    row_wait(gall.at[r], lambda q: gall.at[q], g_s, g_r)
    whole = gall[...].reshape(g["N2"], g["N2"])
    gt[...] = whole.astype(jnp.float32).T.astype(jnp.bfloat16)
    col_wait(mida.at[r, c], lambda q: mida.at[r, q], mq_s, mq_r)
    def cr_wait(k):
        peer = lax.rem(d + k, D)
        rc(csend.at[peer], crecv.at[peer], cr_s.at[k], cr_r.at[peer], peer // nc, lax.rem(peer, nc)).wait()
    each(1, D, cr_wait)
    sums = jnp.sum(crecv[...], axis=0)

    def cg_at(q):
        return cg.at[pl.ds(pl.multiple_of(q * CR, CR), CR)]

    cg[pl.ds(pl.multiple_of(d * CR, CR), CR), :] = sums

    def ca_go(k):
        peer = lax.rem(d + k, D)
        rc(cg_at(d), cg_at(d), ca_s.at[k], ca_r.at[d], peer // nc, lax.rem(peer, nc)).start()
    each(1, D, ca_go)
    mate_slab = rc(mida.at[r], mida.at[r], mf_s.at[0], mf_r.at[r], mate, c)
    pair_slab = rc(mida.at[r], mida.at[r], mf_s.at[1], mf_r.at[r], yp, c)
    pair_slab.start()
    mate_slab.start()
    norm_o[...] = jnp.broadcast_to(jnp.sum(jnp.sum(midc[:, Q1:], axis=0), keepdims=True) * g["norm_scale"], norm_o.shape)
    def ca_wait(k):
        peer = lax.rem(d + k, D)
        rc(cg_at(d), cg_at(peer), ca_s.at[k], ca_r.at[peer], peer // nc, lax.rem(peer, nc)).wait()
    each(1, D, ca_wait)
    rc(mida.at[r], mida.at[yp], mf_s.at[1], mf_r.at[yp], yp, c).wait_recv()
    passed_slab = rc(mida.at[yp], mida.at[yp], mf_s.at[2], mf_r.at[yp], mate, c)
    passed_slab.start()
    halfway = dot(gt[...], cg[...].astype(jnp.bfloat16)).astype(jnp.bfloat16)
    ccoef[...] = dot(gall[...].reshape(g["N2"], g["N2"]), halfway)
    coarse_o[...] = ccoef[pl.ds(pl.multiple_of(r * R2, R2), R2), :]
    coarse_low = ccoef[...].astype(jnp.bfloat16)
    own_rows = pl.ds(pl.multiple_of(c * C1, C1), C1)
    mid_o[...] = 0.5 * midc[:, :Q1].reshape(C1, -1) + g["scale_e2"] * dot(e2t[own_rows, :], coarse_low)
    rc(mida.at[r], mida.at[mate], mf_s.at[0], mf_r.at[mate], mate, c).wait_recv()
    rc(mida.at[yp], mida.at[diag], mf_s.at[2], mf_r.at[diag], mate, c).wait_recv()
    for slab in (mate_slab, pair_slab, passed_slab):
        slab.wait_send()
    for q in range(nc):
        corr = g["scale_e2"] * dot(e2t[q * C1:(q + 1) * C1, :], coarse_low)
        for k in range(nr):
            mcb[q * C1 + k * Q1:q * C1 + (k + 1) * Q1] = (
                0.5 * mida[k, q].astype(jnp.float32) + corr[k * Q1:(k + 1) * Q1]).astype(jnp.bfloat16)
    fine_o[...] = 0.5 * own_vals + g["scale_e1"] * dot(e1own[...], mcb[...])
    for q in range(CHUNKS):
        y_copy(q).wait_send()
        x_copy(q).wait_send()
        f_copy(q).wait_send()
        g_copy(q).wait_send()
    mate_copy.wait_send()


def fits(nr, nc, R0, R1, R2):
    if nr != 4 or nc % nr or (nc // nr) % 2:
        return False
    if R0 % (nc * TILE) or (R1 * nr) % (nc * TILE) or R1 % TILE or 2 * R2 != TILE:
        return False
    if (nr * R2) % (nr * nc * 8) or (nr * R2) % TILE or (nc * TILE) % (nr * R2):
        return False
    return 2 * (R0 // nc) * R0 * nr <= 8 << 20


def fused(values, points0, points1, points2, tiles_a0, tiles_e1, tiles_a1, factor):
    nr, nc = lax.axis_size("row"), lax.axis_size("col")
    R0, R1, R2 = points0.shape[1], points1.shape[1], points2.shape[1]
    F = values.shape[-1]
    if not fits(nr, nc, R0, R1, R2) or F != TILE:
        return per_device(values, points0, points1, points2, tiles_a0, tiles_e1, tiles_a1, factor)
    D, N2 = nr * nc, nr * R2
    T0, T1 = R0 // TILE, R1 // TILE
    B0, B1 = R0 * nr // nc // TILE, R1 * nr // nc // TILE
    S0 = R0 // nc
    I0 = S0 // TILE
    C1, CR, Q1 = B1 * TILE, N2 // D, R1 // nc
    used = 2 * T0 + 2 * T1 + 4
    NP = -(-used // 8) * 8
    NO = I0 * (B0 + B1)
    NOP = -(-NO // 8) * 8
    g = dict(nr=nr, nc=nc, R0=R0, R1=R1, R2=R2, N2=N2,
             scale_a0=(R0 / (nc * tiles_a0.shape[-1] * TILE * TILE)) ** 0.5,
             scale_e1=(R0 / (nc * tiles_e1.shape[-1] * TILE * TILE)) ** 0.5,
             scale_a1=(R1 / (nc * tiles_a1.shape[-1] * TILE * TILE)) ** 0.5,
             scale_e2=(1.0 / (R1 * nr)) ** 0.5,
             norm_scale=1.0 / (R0 * nr * F))
    f32, bf16 = jnp.float32, jnp.bfloat16
    V = pltpu.VMEM
    dma = pltpu.SemaphoreType.DMA
    scratch = [
        V((NP, TILE), f32), V((nc, NOP, TILE), f32), V((R2, TILE), bf16), V((B1 * T0, TILE), f32), V((T1 * B1, TILE), f32),
        V((nr, NP, TILE), f32), V((nc, NOP, TILE), f32), V((nc, R2, TILE), bf16),
        V((nr, R0, F), bf16), V((nr, S0, R0), bf16), V((S0, nr * R1), bf16), V((C1, R0), bf16),
        V((nr * R1, N2), bf16), V((N2, R1 + C1), bf16), V((R1, C1), bf16),
        V((2 * I0, TILE, TILE), f32), V((nr * T1, 2, TILE, TILE), f32), V((2 * N2 // TILE, TILE, TILE), f32),
        V((R0, F), bf16), V((nr, Q1, F), f32), V((nr, Q1, F), f32), V((nr, Q1 + 8, F), f32),
        V((nr, nc, Q1, F), bf16), V((R1 + C1, F), bf16), V((D, CR, F), f32), V((D, CR, F), f32),
        V((N2, F), f32), V((nr, R2, N2), bf16), V((N2, N2), bf16), V((N2, F), f32), V((nr * R1, F), bf16),
    ]
    for n in (nr, nc, nc, CHUNKS, CHUNKS, CHUNKS, CHUNKS, 1, nr, nc, nr, nr, nc, nr, D, D):
        scratch += [dma((n,)), dma((n,))]
    vm = pl.BlockSpec(memory_space=pltpu.VMEM)
    fine, mid, coarse, norm = pl.pallas_call(
        functools.partial(cycle_kernel, g),
        out_shape=(jax.ShapeDtypeStruct((S0, F), f32), jax.ShapeDtypeStruct((C1, F), f32),
                   jax.ShapeDtypeStruct((R2, F), f32), jax.ShapeDtypeStruct((8, TILE), f32)),
        in_specs=[vm] * 8,
        out_specs=[vm] * 4,
        scratch_shapes=scratch,
        compiler_params=pltpu.CompilerParams(collective_id=0, has_side_effects=True, vmem_limit_bytes=48 << 20),
    )(values, points0, points1, points2, tiles_a0, tiles_e1, tiles_a1, factor)
    return (fine, mid, coarse, norm[0, :1])


def solution(mesh):
    return jax.shard_map(
        fused,
        mesh=mesh,
        in_specs=(
            P("row", None),
            P(None, "row"),
            P(None, "row"),
            P(None, "row"),
            P("row", "col", None, None),
            P("row", "col", None, None),
            P("row", "col", None, None),
            P("row", "col"),
        ),
        out_specs=(P(("row", "col"), None), P("col", None), P("row", None), P()),
        check_vma=False,
    )
```

profile of v0, /device:TPU:0, one launch (start us, length us, event | category | flops | bytes accessed | tf_op | source)
XLA Modules:
  0.0 64.0 jit_solution(3294326875388873243)
XLA Ops:
  0.6 0.0 copy-start.5
  0.6 0.0 copy-start.4
  0.7 0.0 copy-start.3
  0.7 0.0 copy-start.6
  0.7 0.0 copy-start.2
  0.7 0.0 copy-start.1
  0.7 0.8 %copy.12.factor = bf16[64,32]{1,0:T(8,128)(2,1)S(1)} copy(bf16[64,32]{0,1:T(8,128)(2,1)} %param.15) | data formatting | bytes 8192 | tf_op args[7]
  1.5 0.0 copy-done.5
  1.5 0.0 copy-done.4
  1.5 0.0 copy-done.3
  1.5 0.0 copy-done.6
  1.6 0.0 copy-done.2
  1.6 0.0 copy-done.1
  1.6 0.0 copy-start
  1.6 1.0 %copy-done = bf16[2048,128]{1,0:T(8,128)(2,1)S(1)} copy-done((bf16[2048,128]{1,0:T(8,128)(2,1)S(1)}, bf16[2048,128]{1,0:T(8,128)(2,1)}, u32[]{:S(2)}) %copy-start) | copy-done | bytes 524312
  2.6 59.0 %shard_map.111 = (f32[256,128]{1,0:T(8,128)S(1)}, f32[256,128]{1,0:T(8,128)S(1)}, f32[64,128]{1,0:T(8,128)S(1)}, f32[8,128]{1,0:T(8,128)S(1)}) custom-call(bf16[2048,128]{1,0:T(8,128)(2,1)S(1)} %copy-done, bf16[2,2048]{1,0:T(2,128)(2,1)S(1)} %copy-done.1, bf16[2,512]{1,0:T(2,128)(2,1)S(1)} %copy-done.2, bf16[2,64]{1,0:T(2,128)(2,1)S(1)} %copy-done.6, ...), custom_call_target="tpu_custom_call" | custom-call | tf_op jit(solution)/shard_map/pallas_call | solution.py:552
  61.6 0.5 slice.3
  62.1 0.7 %copy.16 = f32[256,128]{1,0:T(8,128)} copy(f32[256,128]{1,0:T(8,128)S(1)} %get-tuple-element.16) | data formatting | bytes 262144
  62.8 0.7 %copy.17 = f32[256,128]{1,0:T(8,128)} copy(f32[256,128]{1,0:T(8,128)S(1)} %get-tuple-element.17) | data formatting | bytes 262144
  63.4 0.6 copy.18
Async XLA Ops:
  0.6 0.9 %copy-start.5 = (s32[1,1,2,4]{3,2,1,0:T(2,128)S(1)}, s32[1,1,2,4]{3,2,1,0:T(2,128)}, u32[]{:S(2)}) copy-start(s32[1,1,2,4]{3,2,1,0:T(2,128)} %tiles_a1.1) | copy-start | bytes 100
  0.6 0.9 %copy-start.4 = (s32[1,1,2,20]{3,2,1,0:T(2,128)S(1)}, s32[1,1,2,20]{3,2,1,0:T(2,128)}, u32[]{:S(2)}) copy-start(s32[1,1,2,20]{3,2,1,0:T(2,128)} %tiles_e1.1) | copy-start | bytes 484
  0.7 0.9 %copy-start.3 = (s32[1,1,2,48]{3,2,1,0:T(2,128)S(1)}, s32[1,1,2,48]{3,2,1,0:T(2,128)}, u32[]{:S(2)}) copy-start(s32[1,1,2,48]{3,2,1,0:T(2,128)} %tiles_a0.1) | copy-start | bytes 1156
  0.7 0.9 %copy-start.6 = (bf16[2,64]{1,0:T(2,128)(2,1)S(1)}, bf16[2,64]{1,0:T(2,128)(2,1)}, u32[]{:S(2)}) copy-start(bf16[2,64]{1,0:T(2,128)(2,1)} %points2.1) | copy-start | bytes 772
  0.7 0.9 %copy-start.2 = (bf16[2,512]{1,0:T(2,128)(2,1)S(1)}, bf16[2,512]{1,0:T(2,128)(2,1)}, u32[]{:S(2)}) copy-start(bf16[2,512]{1,0:T(2,128)(2,1)} %points1.1) | copy-start | bytes 6148
  0.7 0.9 %copy-start.1 = (bf16[2,2048]{1,0:T(2,128)(2,1)S(1)}, bf16[2,2048]{1,0:T(2,128)(2,1)}, u32[]{:S(2)}) copy-start(bf16[2,2048]{1,0:T(2,128)(2,1)} %points0.1) | copy-start | bytes 24580
  1.6 1.0 %copy-start = (bf16[2048,128]{1,0:T(8,128)(2,1)S(1)}, bf16[2048,128]{1,0:T(8,128)(2,1)}, u32[]{:S(2)}) copy-start(bf16[2048,128]{1,0:T(8,128)(2,1)} %vals.1) | copy-start | bytes 1572868
where the time goes:
time: 64.2 us; the launch traced here: 64 us
  Pallas kernels  59 us (92%)
  local copies, waits for them, and re-layouts  4.32 us (7%)
  between operations  0.74 us (1%)
    pallas_call x1, Pallas kernels, fused(): pl.pallas_call(functools.partial(cycle_kernel, g), out_shape=(jax.ShapeDt...  59 us
    unnamed x18, local copies, waits for them, and re-layouts  3.81 us

commit v1 on v0

v1 whole, which is shorter than its diff:
```python
import functools
import math

import jax
import jax.numpy as jnp
from jax import lax
from jax.experimental import pallas as pl
from jax.experimental.pallas import tpu as pltpu
from jax.sharding import PartitionSpec as P

TILE = 128


support_fine = 0.35
support_mid = 0.55
support_coarse = 0.8


def spread(x, axis, root):
    mine = lax.axis_index(axis) == root
    return lax.psum(jnp.where(mine, x, jnp.zeros_like(x)), axis)


def wendland(left_pts, right_pts, support):
    left = left_pts.astype(jnp.float32)
    right = right_pts.astype(jnp.float32)
    across = left[0][..., :, None] - right[0][..., None, :]
    upward = left[1][..., :, None] - right[1][..., None, :]
    ratio_t = jnp.sqrt(across * across + upward * upward) / support
    margin = jnp.maximum(1.0 - ratio_t, 0.0)
    squared = margin * margin
    return (squared * squared * (4.0 * ratio_t + 1.0)).astype(jnp.bfloat16)


def listed_terms(row_pts, col_pts, listing, vector, support, flipped):
    row_tiles = row_pts.reshape(2, -1, TILE)
    col_tiles = col_pts.reshape(2, -1, TILE)
    listed = listing.shape[-1]
    group = math.gcd(listed, 32)
    order = listing.reshape(2, listed // group, group)
    fields = vector.shape[-1]
    inputs = vector.reshape(-1, TILE, fields)
    target = col_tiles.shape[1] if flipped else row_tiles.shape[1]
    total = jnp.zeros((target, TILE, fields), jnp.float32)

    def add_group(total, pair):
        tile_rows, tile_cols = pair
        kernel = wendland(row_tiles[:, tile_rows], col_tiles[:, tile_cols], support)
        if flipped:
            contrib = jnp.einsum(
                "gij,gir->gjr", kernel, inputs[tile_rows], preferred_element_type=jnp.float32
            )
            return (total.at[tile_cols].add(contrib), None)
        contrib = jnp.einsum(
            "gij,gjr->gir", kernel, inputs[tile_cols], preferred_element_type=jnp.float32
        )
        return (total.at[tile_rows].add(contrib), None)

    total, unused = lax.scan(add_group, total, (order[0], order[1]))
    return total.reshape(-1, fields)


def per_device(values, points0, points1, points2, tiles_a0, tiles_e1, tiles_a1, factor):
    row_count = lax.axis_size("row")
    col_count = lax.axis_size("col")
    col_id = lax.axis_index("col")
    col_per_row = col_count // row_count
    rows_fine, fields = values.shape
    rows_mid = points1.shape[1]
    share = rows_fine // col_count
    cols_fine = rows_fine // col_per_row
    cols_mid = rows_mid // col_per_row
    source = col_id // col_per_row
    part_index = col_id % col_per_row
    value_piece = lax.dynamic_slice_in_dim(values, part_index * cols_fine, cols_fine, 0)
    fine_piece = lax.dynamic_slice_in_dim(points0, part_index * cols_fine, cols_fine, 1)
    mid_piece = lax.dynamic_slice_in_dim(points1, part_index * cols_mid, cols_mid, 1)
    value_cols, fine_cols, mid_cols = (
        spread(value_piece, "row", source),
        spread(fine_piece, "row", source),
        spread(mid_piece, "row", source),
    )
    scale_a0 = (rows_fine / (col_count * tiles_a0.shape[-1] * TILE * TILE)) ** 0.5
    scale_e1 = (rows_fine / (col_count * tiles_e1.shape[-1] * TILE * TILE)) ** 0.5
    scale_a1 = (rows_mid / (col_count * tiles_a1.shape[-1] * TILE * TILE)) ** 0.5
    scale_e2 = (1.0 / (rows_mid * row_count)) ** 0.5
    fine_data = values.astype(jnp.float32)
    own_data = lax.dynamic_slice_in_dim(values, col_id * share, share, 0).astype(jnp.float32)
    product_part = listed_terms(points0, fine_cols, tiles_a0[0, 0], value_cols, support_fine, False)
    product_whole = lax.psum(product_part, "col")
    fine_residual = fine_data - 0.5 * (scale_a0 * product_whole)
    fine_square = jnp.sum(fine_residual * fine_residual)
    restrict_part = listed_terms(
        points0, mid_cols, tiles_e1[0, 0], fine_residual.astype(jnp.bfloat16), support_mid, True
    )
    restrict_sum = lax.psum(restrict_part, "row")
    mid_data = scale_e1 * restrict_sum
    mid_part = listed_terms(
        points1, mid_cols, tiles_a1[0, 0], mid_data.astype(jnp.bfloat16), support_mid, False
    )
    mid_whole = (scale_a1 * lax.psum(mid_part, "col")).astype(jnp.bfloat16)
    mid_slice = lax.dynamic_slice_in_dim(mid_whole, part_index * cols_mid, cols_mid, 0)
    mid_turned = spread(mid_slice, "row", source)
    mid_residual = mid_data - 0.5 * mid_turned.astype(jnp.float32)
    coarse_kernel = wendland(points2, mid_cols, support_coarse)
    coarse_part = jnp.dot(
        coarse_kernel, mid_residual.astype(jnp.bfloat16), preferred_element_type=jnp.float32
    )
    coarse_sum = lax.psum(coarse_part, "col")
    coarse_data = (scale_e2 * coarse_sum).astype(jnp.bfloat16)
    halfway_part = lax.dot_general(
        factor, coarse_data, (((0,), (0,)), ((), ())), preferred_element_type=jnp.float32
    )
    halfway = lax.psum(halfway_part, "row").astype(jnp.bfloat16)
    coarse_part_two = jnp.dot(factor, halfway, preferred_element_type=jnp.float32)
    coarse_coef = lax.psum(coarse_part_two, "col")
    prolong_part = lax.dot_general(
        coarse_kernel,
        coarse_coef.astype(jnp.bfloat16),
        (((0,), (0,)), ((), ())),
        preferred_element_type=jnp.float32,
    )
    mid_coef = 0.5 * mid_data + scale_e2 * lax.psum(prolong_part, "row")
    fine_part = listed_terms(
        points0, mid_cols, tiles_e1[0, 0], mid_coef.astype(jnp.bfloat16), support_mid, False
    )
    fine_coef = 0.5 * own_data + scale_e1 * lax.psum_scatter(
        fine_part, "col", scatter_dimension=0, tiled=True
    )
    fine_total = lax.psum(fine_square / col_count, ("row", "col"))
    fine_norm = fine_total / (rows_fine * row_count * fields)
    return (fine_coef, mid_coef, coarse_coef, jnp.stack([fine_norm]))


FAR = 1024.0
CHUNKS = 4
MESH = pl.DeviceIdType.MESH


def phi_tile(cx, cy, rx, ry, inv_square):
    across = cx - rx
    upward = cy - ry
    square = (across * across + upward * upward) * inv_square
    t = square * lax.rsqrt(jnp.maximum(square, 1e-30))
    margin = jnp.maximum(1.0 - t, 0.0)
    squared = margin * margin
    return (squared * squared * (4.0 * t + 1.0)).astype(jnp.bfloat16)


def dot(a, b):
    return jnp.dot(a, b, preferred_element_type=jnp.float32)


def far_rows(tiles, row_tiles, col_tiles, by_col):
    row, col = tiles[0, 0, 0:1, :], tiles[0, 0, 1:2, :]
    key = col * row_tiles + row if by_col else row * col_tiles + col
    count = row_tiles * col_tiles
    place = lax.broadcasted_iota(jnp.int32, (count, key.shape[1]), 0)
    near = jnp.max(jnp.where(place == key, 1.0, 0.0), axis=1, keepdims=True)
    return jnp.broadcast_to(FAR * (1.0 - near), (count, TILE))


def halves(x):
    high = x.astype(jnp.bfloat16)
    return high, (x - high.astype(jnp.float32)).astype(jnp.bfloat16)


def cycle_kernel(g, vals_h, points0_h, points1_h, points2_h, tiles_a0_h, tiles_e1_h, tiles_a1_h, factor_h,
                 fine_o, mid_o, coarse_o, norm_o,
                 points0, points1, points2, tiles_a0, tiles_e1, tiles_a1, factor,
                 pts, offs, fac, offe, offa, ptsg, offg, facg, offag, gtg, vall, a0, e1own, e1t, e2t, a1t, cf, cm, cc2,
                 resg, part_buf, rsin, midc, mida, csend, crecv, cg, wcat, zcat, mcb,
                 l_s, p_m, o_m, f_m, oa_m, g_m, v_s, vy_r, vx_r, vg_r, vp_r, re_s, rez_r, rex_r,
                 rs_m, mc_m, mq_m, mf_s, mf_r, cr_m, ca_m):
    nr, nc, R0, R1, R2 = g["nr"], g["nc"], g["R0"], g["R1"], g["R2"]
    D = nr * nc
    T0, T1 = R0 // TILE, R1 // TILE
    C0, C1 = R0 * nr // nc, R1 * nr // nc
    B0, B1 = C0 // TILE, C1 // TILE
    S0 = R0 // nc
    I0 = S0 // TILE
    Q1 = C1 // nr
    N2 = g["N2"]
    CR = N2 // D
    NT1 = nr * T1
    NT2 = N2 // TILE
    X1, Y1, X2 = 2 * T0, 2 * T0 + T1, 2 * T0 + 2 * T1
    fine_inv, mid_inv, coarse_inv = (1.0 / (s * s) for s in (support_fine, support_mid, support_coarse))
    r = lax.axis_index("row")
    c = lax.axis_index("col")
    d = r * nc + c
    mate = r + 1 - 2 * lax.rem(r, 2)
    yp = lax.rem(r + 2, nr)
    diag = lax.rem(mate + 2, nr)
    h = lax.rem(c, 2)
    xp = c + 1 - 2 * h

    def rc(src, dst, ssem, rsem, rr, cc):
        return pltpu.make_async_remote_copy(src_ref=src, dst_ref=dst, send_sem=ssem, recv_sem=rsem,
                                            device_id=(rr, cc), device_id_type=MESH)

    def each(lo, hi, f):
        def body(k, carry):
            f(k)
            return carry
        lax.fori_loop(lo, hi, body, 0)

    barrier = pltpu.get_barrier_semaphore()

    def greet(k):
        q = lax.rem(c + k, nc)
        for j in range(nr):
            pl.semaphore_signal(barrier, inc=1, device_id=(lax.rem(r + j, nr), q), device_id_type=MESH)

    each(1, nc, greet)
    for j in range(1, nr):
        pl.semaphore_signal(barrier, inc=1, device_id=(lax.rem(r + j, nr), c), device_id_type=MESH)
    loads = [pltpu.make_async_copy(s, t, l_s.at[k]) for k, (s, t) in enumerate((
        (points0_h, points0), (points1_h, points1), (points2_h, points2), (tiles_a0_h, tiles_a0),
        (tiles_e1_h, tiles_e1), (tiles_a1_h, tiles_a1), (factor_h, factor), (vals_h, vall.at[r])))]
    for load in loads:
        load.start()

    pts[...] = jnp.zeros_like(pts)
    offs[...] = jnp.zeros_like(offs)
    for load in loads[:-1]:
        load.wait()
    for way in range(2):
        for ref, at, count in ((points0, way * T0, T0), (points1, X1 + way * T1, T1)):
            line = ref[way:way + 1, :].astype(jnp.float32)
            for k in range(count):
                pts[at + k:at + k + 1, :] = line[:, k * TILE:(k + 1) * TILE]
        line = points2[way:way + 1, :].astype(jnp.float32)
        blank = jnp.zeros((1, TILE - R2), jnp.float32)
        pts[X2 + way:X2 + way + 1, :] = jnp.concatenate([line, blank], axis=1)
        pts[X2 + 2 + way:X2 + 3 + way, :] = jnp.concatenate([blank, line], axis=1)
    far_a0 = far_rows(tiles_a0, T0, B0, False)
    far_e1 = far_rows(tiles_e1, T0, B1, False)
    for q in range(nc):
        offs[q, :I0 * B0] = far_a0[q * I0 * B0:(q + 1) * I0 * B0]
        offs[q, I0 * B0:I0 * (B0 + B1)] = far_e1[q * I0 * B1:(q + 1) * I0 * B1]
    half_of = lax.rem(r, TILE // R2)
    raw = factor[...].astype(jnp.float32)
    fac[...] = jnp.concatenate([jnp.where(half_of == k, raw, 0.0) for k in range(TILE // R2)], axis=1).astype(jnp.bfloat16)
    offe[...] = far_rows(tiles_e1, T0, B1, True)
    offa[...] = far_rows(tiles_a1, T1, B1, False)
    loads[-1].wait()
    pl.semaphore_wait(barrier, D - 1)

    def row_send(src_of, dst, m):
        for k in range(1, nr):
            q = lax.rem(r + k, nr)
            rc(src_of(q), dst, m.at[0], m.at[1], q, c).start()

    def row_wait(slots, m):
        rc(slots, slots, m.at[0], m.at[1], mate, c).wait()

    def col_send(src_of, dst, m):
        def go(k):
            q = lax.rem(c + k, nc)
            rc(src_of(q), dst, m.at[0], m.at[1], r, q).start()
        each(1, nc, go)

    HALF = R0 // 2
    CH = HALF // CHUNKS

    def chunk(half, q):
        return pl.ds(pl.multiple_of(half * HALF + q * CH, CH), CH)

    def y_copy(q):
        return rc(vall.at[r, chunk(h, q)], vall.at[r, chunk(h, q)], v_s.at[0], vy_r.at[q], yp, c)

    def y_in(q):
        return rc(vall.at[yp, chunk(h, q)], vall.at[yp, chunk(h, q)], v_s.at[0], vy_r.at[q], yp, c)

    def x_copy(q):
        return rc(vall.at[yp, chunk(h, q)], vall.at[yp, chunk(h, q)], v_s.at[0], vx_r.at[q], r, xp)

    def x_in(q):
        return rc(vall.at[yp, chunk(1 - h, q)], vall.at[yp, chunk(1 - h, q)], v_s.at[0], vx_r.at[q], r, xp)

    def g_copy(half, q):
        return rc(vall.at[yp, chunk(half, q)], vall.at[yp, chunk(half, q)], v_s.at[0], vg_r.at[0], mate, c)

    row_send(lambda q: pts, ptsg.at[r], p_m)
    col_send(lambda q: offs.at[q], offg.at[c], o_m)
    for q in range(CHUNKS):
        y_copy(q).start()
    rc(vall.at[r], vall.at[r], v_s.at[0], vp_r.at[0], mate, c).start()
    row_send(lambda q: offa, offag.at[r], oa_m)
    row_send(lambda q: fac, facg.at[r], f_m)
    ptsg[r] = pts[...]
    offg[c] = offs[c]
    offag[r] = offa[...]
    facg[r] = fac[...]

    def turned(row):
        return jnp.broadcast_to(row, (TILE, TILE)).T

    for i in range(I0):
        for way in range(2):
            cf[2 * i + way] = turned(pts[pl.ds(way * T0 + c * I0 + i, 1), :])
    row_wait(ptsg.at[pl.ds(0, nr - 1)], p_m)

    def turn_mid(k):
        for way in range(2):
            cm[k, way] = turned(ptsg[k // T1, pl.ds(X1 + way * T1 + lax.rem(k, T1), 1), :])
    each(0, NT1, turn_mid)
    rc(offg.at[pl.ds(0, nc - 1)], offg.at[pl.ds(0, nc - 1)], o_m.at[0], o_m.at[1], r, xp).wait()

    blocks = (r, mate, yp, diag)
    for s, rb in enumerate(blocks):
        def build_a0(kk, s=s, rb=rb):
            rx = ptsg[rb, pl.ds(kk, 1), :]
            ry = ptsg[rb, pl.ds(T0 + kk, 1), :]
            cb = rb * (nc // nr) + kk // B0
            j = lax.rem(kk, B0)
            for i in range(I0):
                off = offg[cb, pl.ds(i * B0 + j, 1), :]
                a0[s, i * TILE:(i + 1) * TILE, pl.ds(pl.multiple_of(kk * TILE, TILE), TILE)] = phi_tile(
                    cf[2 * i], cf[2 * i + 1], rx + off, ry, fine_inv)
        each(0, T0, build_a0)
        if s < CHUNKS:
            y_in(s).wait_recv()
            x_copy(s).start()
            g_copy(h, s).start()
    acc = dot(a0[0], vall[r])
    for q in range(CHUNKS):
        x_in(q).wait_recv()
        g_copy(1 - h, q).start()
    rc(vall.at[mate], vall.at[mate], v_s.at[0], vp_r.at[0], mate, c).wait_recv()
    acc = acc + dot(a0[1], vall[mate])
    acc = acc + dot(a0[2], vall[yp])
    rc(vall.at[diag], vall.at[diag], v_s.at[0], vg_r.at[0], mate, c).wait_recv()
    acc = acc + dot(a0[3], vall[diag])
    own_vals = vall[r, pl.ds(pl.multiple_of(c * S0, S0), S0), :].astype(jnp.float32)
    res = own_vals - (0.5 * g["scale_a0"]) * acc

    def res_at(q):
        return resg.at[pl.ds(pl.multiple_of(q * S0, S0), S0)]

    resg[pl.ds(pl.multiple_of(c * S0, S0), S0), :] = res.astype(jnp.bfloat16)
    for k in range(1, nc // 2):
        q = lax.rem(c + 2 * k, nc)
        rc(res_at(c), res_at(c), re_s.at[0], rez_r.at[nc // 2 - k], r, q).start()
    rc(res_at(c), res_at(c), re_s.at[0], rex_r.at[0], r, xp).start()

    def res_pass(k):
        q = lax.rem(c + 2 * k, nc)
        rc(res_at(q), res_at(q), re_s.at[0], rez_r.at[k], r, q).wait_recv()
        rc(res_at(q), res_at(q), re_s.at[0], rex_r.at[0], r, xp).start()

    def build_e1t(i):
        rx, ry = pts[pl.ds(i, 1), :], pts[pl.ds(T0 + i, 1), :]
        for j in range(B1):
            off = offe[pl.ds(j * T0 + i, 1), :]
            e1t[j * TILE:(j + 1) * TILE, pl.ds(pl.multiple_of(i * TILE, TILE), TILE)] = phi_tile(
                cm[c * B1 + j, 0], cm[c * B1 + j, 1], rx + off, ry, mid_inv)
    each(0, T0, build_e1t)
    row_wait(facg.at[pl.ds(0, nr - 1)], f_m)
    strips = []
    per = TILE // R2
    for lane in range(N2 // TILE):
        total = facg[lane * per].astype(jnp.float32)
        for k in range(1, per):
            total = total + facg[lane * per + k].astype(jnp.float32)
        strips.append(total)
    gtg[c] = jnp.concatenate(strips, axis=1).astype(jnp.bfloat16)
    col_send(lambda q: gtg.at[c], gtg.at[c], g_m)

    def coarse_row(t, way):
        return ptsg[per * t, X2 + way:X2 + way + 1, :] + ptsg[per * t + 1, X2 + 2 + way:X2 + 3 + way, :]

    for t in range(NT2):
        for way in range(2):
            cc2[2 * t + way] = jnp.broadcast_to(coarse_row(t, way), (8, TILE))
    res_pass(1)

    def build_e2t(k):
        for t in range(NT2):
            e2t[pl.ds(pl.multiple_of(k * TILE, TILE), TILE), t * TILE:(t + 1) * TILE] = phi_tile(
                cm[k, 0], cm[k, 1], cc2[2 * t, 0:1], cc2[2 * t + 1, 0:1], coarse_inv)
    each(0, NT1, build_e2t)
    res_pass(nc // 2 - 1)
    row_wait(offag.at[pl.ds(0, nr - 1)], oa_m)
    own_tile = c * B1 + (r * Q1) // TILE
    own_half = pl.ds(pl.multiple_of(lax.rem(r * Q1, TILE), Q1), Q1)
    ox, oy = cm[own_tile, 0, own_half, :], cm[own_tile, 1, own_half, :]

    def build_a1t(k):
        rx = ptsg[k // T1, pl.ds(X1 + lax.rem(k, T1), 1), :]
        ry = ptsg[k // T1, pl.ds(Y1 + lax.rem(k, T1), 1), :]
        off = offag[k // T1, pl.ds(lax.rem(k, T1) * B1 + (r * Q1) // TILE, 1), :]
        a1t[:, pl.ds(pl.multiple_of(k * TILE, TILE), TILE)] = phi_tile(ox, oy, rx + off, ry, mid_inv)
    each(0, NT1, build_a1t)
    own_mids = pl.ds(pl.multiple_of(c * C1 + r * Q1, Q1), Q1)
    turned_w = g["scale_e2"] * (e2t[own_mids, :].astype(jnp.float32)
                                - (0.5 * g["scale_a1"]) * dot(a1t[...], e2t[...]))
    w_high, w_low = halves(turned_w)
    w_pair = jnp.concatenate([w_high.astype(jnp.float32), w_low.astype(jnp.float32)], axis=0).T.astype(jnp.bfloat16)
    wcat[:, :TILE] = w_pair
    wcat[:, TILE:] = w_pair
    for k in range(2, nc // 2 - 1):
        res_pass(k)

    def build_e1own(k):
        rx = ptsg[k // T1, pl.ds(X1 + lax.rem(k, T1), 1), :]
        ry = ptsg[k // T1, pl.ds(Y1 + lax.rem(k, T1), 1), :]
        for i in range(I0):
            off = offg[k // B1, pl.ds(I0 * B0 + i * B1 + lax.rem(k, B1), 1), :]
            e1own[i * TILE:(i + 1) * TILE, pl.ds(pl.multiple_of(k * TILE, TILE), TILE)] = phi_tile(
                cf[2 * i], cf[2 * i + 1], rx + off, ry, mid_inv)
    each(0, NT1, build_e1own)

    rc(resg.at[pl.ds(0, (nc // 2) * S0)], resg.at[pl.ds(0, (nc // 2) * S0)], re_s.at[0], rex_r.at[0], r, xp).wait_recv()
    held = resg[...].astype(jnp.float32)
    square = jnp.sum((held * held).reshape(R0 // 8, 8, -1), axis=0)
    part_buf[...] = dot(e1t[...], resg[...]).reshape(nr, Q1, -1)
    row_send(lambda q: part_buf.at[q], rsin.at[r], rs_m)
    rsin[r] = part_buf[r]
    rc(gtg.at[pl.ds(0, nc - 1)], gtg.at[pl.ds(0, nc - 1)], g_m.at[0], g_m.at[1], r, xp).wait()
    gt = gtg[...].reshape(N2, N2)
    gg_high, gg_low = halves(dot(gt.astype(jnp.float32).T.astype(jnp.bfloat16), gt))
    zcat[2 * C1:, :N2] = gg_high
    zcat[2 * C1:, N2:] = gg_low
    h_high, h_low = halves((g["scale_e1"] * g["scale_e2"]) * dot(e1own[...], e2t[...]))
    steps = (dot(h_high, gg_high) + dot(h_low, gg_high) + dot(h_high, gg_low),)
    own_rows = pl.ds(pl.multiple_of(c * C1, C1), C1)
    rows_c = e2t[own_rows, :]
    steps += (g["scale_e2"] * (dot(rows_c, gg_high) + dot(rows_c, gg_low)),)
    for k, step in enumerate(steps):
        high, low = halves(step)
        zcat[k * C1:(k + 1) * C1, :N2] = high
        zcat[k * C1:(k + 1) * C1, N2:] = low

    row_wait(rsin.at[pl.ds(0, nr - 1)], rs_m)
    quarter = rsin[0]
    for k in range(1, nr):
        quarter = quarter + rsin[k]
    quarter = g["scale_e1"] * quarter
    q_high, q_low = halves(quarter)
    part = dot(wcat[...], jnp.concatenate([q_high, q_high, q_low, q_low], axis=0))
    csend[...] = part.reshape(D, CR, -1).astype(jnp.bfloat16)

    def all_send(src_of, dst, m):
        def go(k):
            q = lax.rem(c + k, nc)
            for j in range(nr):
                p = lax.rem(r + j, nr)
                rc(src_of(p * nc + q), dst, m.at[0], m.at[1], p, q).start()
        each(1, nc, go)
        for j in range(1, nr):
            p = lax.rem(r + j, nr)
            rc(src_of(p * nc + c), dst, m.at[0], m.at[1], p, c).start()

    def all_wait(ref, m):
        rc(ref.at[pl.ds(0, D - 1)], ref.at[pl.ds(0, D - 1)], m.at[0], m.at[1], mate, c).wait()

    all_send(lambda q: csend.at[q], crecv.at[d], cr_m)
    midc[r] = jnp.concatenate([quarter, square], axis=0)
    mida[r, c] = q_high
    col_send(lambda q: mida.at[r, c], mida.at[r, c], mq_m)
    row_send(lambda q: midc.at[r], midc.at[r], mc_m)
    crecv[d] = csend[d]
    rc(mida.at[r, pl.ds(0, nc - 1)], mida.at[r, pl.ds(0, nc - 1)], mq_m.at[0], mq_m.at[1], r, xp).wait()
    all_wait(crecv, cr_m)
    cg[d] = jnp.sum(crecv[...].astype(jnp.float32), axis=0).astype(jnp.bfloat16)
    all_send(lambda q: cg.at[d], cg.at[d], ca_m)
    rc(mida.at[r], mida.at[r], mf_s.at[0], mf_r.at[0], yp, c).start()
    rc(mida.at[r], mida.at[r], mf_s.at[0], mf_r.at[1], mate, c).start()
    row_wait(midc.at[pl.ds(0, nr - 1)], mc_m)
    norm_o[...] = jnp.broadcast_to(jnp.sum(jnp.sum(midc[:, Q1:], axis=0), keepdims=True) * g["norm_scale"], norm_o.shape)
    rc(mida.at[yp], mida.at[yp], mf_s.at[0], mf_r.at[0], yp, c).wait_recv()
    rc(mida.at[yp], mida.at[yp], mf_s.at[0], mf_r.at[2], mate, c).start()
    all_wait(cg, ca_m)
    cd = cg[...].astype(jnp.float32).reshape(N2, -1).astype(jnp.bfloat16)
    both = jnp.concatenate([cd, cd], axis=0)
    mid_o[...] = 0.5 * midc[:, :Q1].reshape(C1, -1) + dot(zcat[C1:2 * C1, :], both)
    coarse_o[...] = dot(zcat[pl.ds(pl.multiple_of(2 * C1 + r * R2, R2), R2), :], both)
    rc(mida.at[mate], mida.at[mate], mf_s.at[0], mf_r.at[1], mate, c).wait_recv()
    rc(mida.at[diag], mida.at[diag], mf_s.at[0], mf_r.at[2], mate, c).wait_recv()
    for q in range(nc):
        for k in range(nr):
            mcb[q * C1 + k * Q1:q * C1 + (k + 1) * Q1] = mida[k, q]
    fine_o[...] = (0.5 * own_vals + (0.5 * g["scale_e1"]) * dot(e1own[...], mcb[...])
                   + dot(zcat[:C1, :], both))
    rc(mida.at[pl.ds(0, nr - 1)], mida.at[pl.ds(0, nr - 1)], mf_s.at[0], mf_r.at[0], mate, c).wait_send()
    rc(vall.at[pl.ds(0, nr - 1)], vall.at[pl.ds(0, nr - 1)], v_s.at[0], vp_r.at[0], mate, c).wait_send()
    rc(resg.at[pl.ds(0, (nc - 1) * S0)], resg.at[pl.ds(0, (nc - 1) * S0)], re_s.at[0], rex_r.at[0], r, xp).wait_send()


def finish_kernel(fine, mid, coarse, norm, fine_o, mid_o, coarse_o, norm_o):
    fine_o[...] = fine[...]
    mid_o[...] = mid[...]
    coarse_o[...] = coarse[...]
    norm_o[...] = norm[0:1, 0:1]


def fits(nr, nc, R0, R1, R2):
    if nr != 4 or nc % nr or (nc // nr) % 2:
        return False
    if 4 * (R1 // nc) != 2 * TILE or R0 != R1 * nr or R0 % (nc * TILE) or (R1 * nr) % (nc * TILE) or R1 % TILE or 2 * R2 != TILE:
        return False
    if (nr * R2) % (nr * nc * 8) or (nr * R2) % TILE or (nc * TILE) % (nr * R2):
        return False
    return 2 * (R0 // nc) * R0 * nr <= 8 << 20


def fused(values, points0, points1, points2, tiles_a0, tiles_e1, tiles_a1, factor):
    nr, nc = lax.axis_size("row"), lax.axis_size("col")
    R0, R1, R2 = points0.shape[1], points1.shape[1], points2.shape[1]
    F = values.shape[-1]
    if not fits(nr, nc, R0, R1, R2) or F != TILE:
        return per_device(values, points0, points1, points2, tiles_a0, tiles_e1, tiles_a1, factor)
    D, N2 = nr * nc, nr * R2
    T0, T1 = R0 // TILE, R1 // TILE
    B0, B1 = R0 * nr // nc // TILE, R1 * nr // nc // TILE
    S0 = R0 // nc
    I0 = S0 // TILE
    C1, CR, Q1 = B1 * TILE, N2 // D, R1 * nr // nc // nr
    used = 2 * T0 + 2 * T1 + 4
    NP = -(-used // 8) * 8
    NO = I0 * (B0 + B1)
    NOP = -(-NO // 8) * 8
    g = dict(nr=nr, nc=nc, R0=R0, R1=R1, R2=R2, N2=N2,
             scale_a0=(R0 / (nc * tiles_a0.shape[-1] * TILE * TILE)) ** 0.5,
             scale_e1=(R0 / (nc * tiles_e1.shape[-1] * TILE * TILE)) ** 0.5,
             scale_a1=(R1 / (nc * tiles_a1.shape[-1] * TILE * TILE)) ** 0.5,
             scale_e2=(1.0 / (R1 * nr)) ** 0.5,
             norm_scale=1.0 / (R0 * nr * F))
    f32, bf16, i32 = jnp.float32, jnp.bfloat16, jnp.int32
    V = pltpu.VMEM
    dma = pltpu.SemaphoreType.DMA
    wide = N2 // nc
    scratch = [
        V(points0.shape, bf16), V(points1.shape, bf16), V(points2.shape, bf16),
        V(tiles_a0.shape, i32), V(tiles_e1.shape, i32), V(tiles_a1.shape, i32), V((wide, R2), bf16),
        V((NP, TILE), f32), V((nc, NOP, TILE), f32), V((wide, TILE), bf16), V((B1 * T0, TILE), f32), V((T1 * B1, TILE), f32),
        V((nr, NP, TILE), f32), V((nc, NOP, TILE), f32), V((nr, wide, TILE), bf16), V((nr, T1 * B1, TILE), f32),
        V((nc, wide, N2), bf16),
        V((nr, R0, F), bf16), V((nr, S0, R0), bf16), V((S0, nr * R1), bf16), V((C1, R0), bf16),
        V((nr * R1, N2), bf16), V((Q1, nr * R1), bf16),
        V((2 * I0, TILE, TILE), f32), V((nr * T1, 2, TILE, TILE), f32), V((2 * N2 // TILE, 8, TILE), f32),
        V((R0, F), bf16), V((nr, Q1, F), f32), V((nr, Q1, F), f32), V((nr, Q1 + 8, F), f32),
        V((nr, nc, Q1, F), bf16), V((D, CR, F), bf16), V((D, CR, F), bf16), V((D, CR, F), bf16),
        V((N2, 4 * Q1), bf16), V((2 * C1 + N2, 2 * N2), bf16), V((nr * R1, F), bf16),
    ]
    for n in (8, 2, 2, 2, 2, 2, 1, CHUNKS, CHUNKS, 1, 1, 1, nc // 2, 1, 2, 2, 2, 1, 3, 2, 2):
        scratch += [dma((n,))]
    vm = pl.BlockSpec(memory_space=pltpu.VMEM)
    shapes = ((S0, F), (C1, F), (R2, F))
    parts = pl.pallas_call(
        functools.partial(cycle_kernel, g),
        out_shape=tuple(jax.ShapeDtypeStruct(s, f32) for s in shapes + ((8, TILE),)),
        in_specs=[pl.BlockSpec(memory_space=pltpu.HBM)] * 8,
        out_specs=[vm] * 4,
        scratch_shapes=scratch,
        compiler_params=pltpu.CompilerParams(collective_id=0, has_side_effects=True, vmem_limit_bytes=48 << 20),
    )(values, points0, points1, points2, tiles_a0, tiles_e1, tiles_a1, factor.T)
    fine, mid, coarse, norm = pl.pallas_call(
        finish_kernel,
        grid=(1,),
        out_shape=tuple(jax.ShapeDtypeStruct(s, f32) for s in shapes + ((1, 1),)),
        in_specs=[vm] * 4,
        out_specs=[pl.BlockSpec(s, lambda i: (0, 0)) for s in shapes + ((1, 1),)],
    )(*parts)
    return (fine, mid, coarse, norm.reshape(1))


def solution(mesh):
    return jax.shard_map(
        fused,
        mesh=mesh,
        in_specs=(
            P("row", None),
            P(None, "row"),
            P(None, "row"),
            P(None, "row"),
            P("row", "col", None, None),
            P("row", "col", None, None),
            P("row", "col", None, None),
            P("row", "col"),
        ),
        out_specs=(P(("row", "col"), None), P("col", None), P("row", None), P()),
        check_vma=False,
    )
```

time: 64.2 us -> 62.6 us (0.975)
  Pallas kernels: 59 us -> 54 us
  local copies, waits for them, and re-layouts: 4.32 us -> 7.61 us
    pallas_call x1 -> x2, Pallas kernels: 59 us -> 54 us  [the longest x1 52.3 us: fused(): pl.pallas_call(functools.partial(cycle_kernel, g), out_shape=tuple((jax.S...]
    unnamed x18 -> x24, local copies, waits for them, and re-layouts: 3.81 us -> 7.61 us
where the time goes in v1:
time: 62.6 us; the launch traced here: 62.3 us
  Pallas kernels  54 us (86%)
  local copies, waits for them, and re-layouts  7.61 us (12%)
  between operations  0.68 us (1%)
    pallas_call x1, Pallas kernels, fused(): pl.pallas_call(functools.partial(cycle_kernel, g), out_shape=tuple((jax.S...  52.3 us
    unnamed x24, local copies, waits for them, and re-layouts  7.61 us
    pallas_call x1, Pallas kernels, fused(): pl.pallas_call(finish_kernel, grid=(1,), out_shape=tuple((jax.ShapeDtypeS...  1.68 us

profile of v1, /device:TPU:0, one launch (start us, length us, event | category | flops | bytes accessed | tf_op | source)
XLA Modules:
  0.0 62.3 jit_solution(16995870212656331557)
XLA Ops:
  0.6 0.0 copy-start.8
  0.6 0.0 copy-start.11
  0.7 0.7 %copy-done.8 = s32[1,1,2,48]{3,2,1,0:T(2,128)S(1)} copy-done((s32[1,1,2,48]{3,2,1,0:T(2,128)S(1)}, s32[1,1,2,48]{3,2,1,0:T(2,128)}, u32[]{:S(2)}) %copy-start.8) | copy-done | bytes 408
  1.3 0.0 copy-done.11
  1.3 0.0 copy-start
  1.3 1.0 %copy-done = bf16[2048,128]{1,0:T(8,128)(2,1)S(1)} copy-done((bf16[2048,128]{1,0:T(8,128)(2,1)S(1)}, bf16[2048,128]{1,0:T(8,128)(2,1)}, u32[]{:S(2)}) %copy-start) | copy-done | bytes 524312
  2.4 0.0 copy-start.4
  2.4 0.7 %copy-done.4 = bf16[2,2048]{1,0:T(2,128)(2,1)S(1)} copy-done((bf16[2,2048]{1,0:T(2,128)(2,1)S(1)}, bf16[2,2048]{1,0:T(2,128)(2,1)}, u32[]{:S(2)}) %copy-start.4) | copy-done | bytes 8216
  3.1 0.0 copy-start.5
  3.1 0.7 %copy-done.5 = bf16[64,32]{0,1:T(8,128)(2,1)S(1)} copy-done((bf16[64,32]{0,1:T(8,128)(2,1)S(1)}, bf16[64,32]{0,1:T(8,128)(2,1)}, u32[]{:S(2)}) %copy-start.5) | copy-done | bytes 4120
  3.8 0.0 copy-start.7
  3.8 0.7 %copy-done.7 = bf16[2,512]{1,0:T(2,128)(2,1)S(1)} copy-done((bf16[2,512]{1,0:T(2,128)(2,1)S(1)}, bf16[2,512]{1,0:T(2,128)(2,1)}, u32[]{:S(2)}) %copy-start.7) | copy-done | bytes 2072
  4.4 0.0 copy-start.9
  4.4 0.7 %copy-done.9 = s32[1,1,2,20]{3,2,1,0:T(2,128)S(1)} copy-done((s32[1,1,2,20]{3,2,1,0:T(2,128)S(1)}, s32[1,1,2,20]{3,2,1,0:T(2,128)}, u32[]{:S(2)}) %copy-start.9) | copy-done | bytes 184
  5.1 0.0 copy-start.10
  5.1 0.7 %copy-done.10 = s32[1,1,2,4]{3,2,1,0:T(2,128)S(1)} copy-done((s32[1,1,2,4]{3,2,1,0:T(2,128)S(1)}, s32[1,1,2,4]{3,2,1,0:T(2,128)}, u32[]{:S(2)}) %copy-start.10) | copy-done | bytes 56
  5.8 52.3 %shard_map.111 = (f32[256,128]{1,0:T(8,128)S(1)}, f32[256,128]{1,0:T(8,128)S(1)}, f32[64,128]{1,0:T(8,128)S(1)}, f32[8,128]{1,0:T(8,128)S(1)}) custom-call(bf16[2048,128]{1,0:T(8,128)(2,1)S(1)} %copy-done, bf16[2,2048]{1,0:T(2,128)(2,1)S(1)} %copy-done.4, bf16[2,512]{1,0:T(2,128)(2,1)S(1)} %copy-done.7, bf16[2,64]{1,0:T(2,128)(2,1)S(1)} %copy-done.11, ...), custom_call_target="tpu_custom_call" | custom-call | tf_op jit(solution)/shard_map/pallas_call | solution.py:552
  58.1 0.0 copy-start.1
  58.1 0.6 %copy-done.1 = f32[256,128]{1,0:T(8,128)} copy-done((f32[256,128]{1,0:T(8,128)}, f32[256,128]{1,0:T(8,128)S(1)}, u32[]{:S(2)}) %copy-start.1) | copy-done | bytes 131096
  58.8 0.0 copy-start.2
  58.8 0.6 %copy-done.2 = f32[256,128]{1,0:T(8,128)} copy-done((f32[256,128]{1,0:T(8,128)}, f32[256,128]{1,0:T(8,128)S(1)}, u32[]{:S(2)}) %copy-start.2) | copy-done | bytes 131096
  59.4 0.6 copy-done.3
  60.0 0.6 copy-done.6
  60.6 1.7 %shard_map.112 = (f32[256,128]{1,0:T(8,128)}, f32[256,128]{1,0:T(8,128)}, f32[64,128]{1,0:T(8,128)}, f32[1,1]{1,0:T(1,128)}) custom-call(f32[256,128]{1,0:T(8,128)} %copy-done.1, f32[256,128]{1,0:T(8,128)} %copy-done.2, f32[64,128]{1,0:T(8,128)} %copy-done.3, f32[8,128]{1,0:T(8,128)} %copy-done.6), custom_call_target="tpu_custom_call" | custom-call | tf_op jit(solution)/shard_map/pallas_call | solution.py:560
  (2 shorter events, 0.0 us)
Async XLA Ops:
  0.6 0.7 %copy-start.8 = (s32[1,1,2,48]{3,2,1,0:T(2,128)S(1)}, s32[1,1,2,48]{3,2,1,0:T(2,128)}, u32[]{:S(2)}) copy-start(s32[1,1,2,48]{3,2,1,0:T(2,128)} %tiles_a0_h.1) | copy-start | bytes 1156
  0.6 0.7 %copy-start.11 = (bf16[2,64]{1,0:T(2,128)(2,1)S(1)}, bf16[2,64]{1,0:T(2,128)(2,1)}, u32[]{:S(2)}) copy-start(bf16[2,64]{1,0:T(2,128)(2,1)} %points2_h.1) | copy-start | bytes 772
  1.3 1.0 %copy-start = (bf16[2048,128]{1,0:T(8,128)(2,1)S(1)}, bf16[2048,128]{1,0:T(8,128)(2,1)}, u32[]{:S(2)}) copy-start(bf16[2048,128]{1,0:T(8,128)(2,1)} %vals_h.1) | copy-start | bytes 1572868
  2.4 0.7 %copy-start.4 = (bf16[2,2048]{1,0:T(2,128)(2,1)S(1)}, bf16[2,2048]{1,0:T(2,128)(2,1)}, u32[]{:S(2)}) copy-start(bf16[2,2048]{1,0:T(2,128)(2,1)} %points0_h.1) | copy-start | bytes 24580
  3.1 0.7 %copy-start.5 = (bf16[64,32]{0,1:T(8,128)(2,1)S(1)}, bf16[64,32]{0,1:T(8,128)(2,1)}, u32[]{:S(2)}) copy-start(bf16[64,32]{0,1:T(8,128)(2,1)} %param.15) | copy-start | bytes 12292
  3.8 0.7 %copy-start.7 = (bf16[2,512]{1,0:T(2,128)(2,1)S(1)}, bf16[2,512]{1,0:T(2,128)(2,1)}, u32[]{:S(2)}) copy-start(bf16[2,512]{1,0:T(2,128)(2,1)} %points1_h.1) | copy-start | bytes 6148
  4.4 0.7 %copy-start.9 = (s32[1,1,2,20]{3,2,1,0:T(2,128)S(1)}, s32[1,1,2,20]{3,2,1,0:T(2,128)}, u32[]{:S(2)}) copy-start(s32[1,1,2,20]{3,2,1,0:T(2,128)} %tiles_e1_h.1) | copy-start | bytes 484
  5.1 0.7 %copy-start.10 = (s32[1,1,2,4]{3,2,1,0:T(2,128)S(1)}, s32[1,1,2,4]{3,2,1,0:T(2,128)}, u32[]{:S(2)}) copy-start(s32[1,1,2,4]{3,2,1,0:T(2,128)} %tiles_a1_h.1) | copy-start | bytes 100
  58.1 0.7 %copy-start.1 = (f32[256,128]{1,0:T(8,128)}, f32[256,128]{1,0:T(8,128)S(1)}, u32[]{:S(2)}) copy-start(f32[256,128]{1,0:T(8,128)S(1)} %get-tuple-element.12.fine) | copy-start | bytes 393220
  58.8 0.6 %copy-start.2 = (f32[256,128]{1,0:T(8,128)}, f32[256,128]{1,0:T(8,128)S(1)}, u32[]{:S(2)}) copy-start(f32[256,128]{1,0:T(8,128)S(1)} %get-tuple-element.13.mid) | copy-start | bytes 393220
  59.4 0.6 copy-start.3
  60.0 0.6 copy-start.6

commit v2 on v1

--- a/solution.py
+++ b/solution.py
@@ -556,13 +556,15 @@
         out_specs=[vm] * 4,
         scratch_shapes=scratch,
         compiler_params=pltpu.CompilerParams(collective_id=0, has_side_effects=True, vmem_limit_bytes=48 << 20),
-    )(values, points0, points1, points2, tiles_a0, tiles_e1, tiles_a1, factor.T)
+    )(*[pltpu.with_memory_space_constraint(x, pltpu.HBM) for x in (
+        values, points0, points1, points2, tiles_a0, tiles_e1, tiles_a1, factor.T)])
     fine, mid, coarse, norm = pl.pallas_call(
         finish_kernel,
         grid=(1,),
         out_shape=tuple(jax.ShapeDtypeStruct(s, f32) for s in shapes + ((1, 1),)),
         in_specs=[vm] * 4,
         out_specs=[pl.BlockSpec(s, lambda i: (0, 0)) for s in shapes + ((1, 1),)],
+        compiler_params=pltpu.CompilerParams(vmem_limit_bytes=4 << 20),
     )(*parts)
     return (fine, mid, coarse, norm.reshape(1))
 

time: 62.6 us -> 54 us (0.86)
  local copies, waits for them, and re-layouts: 7.61 us -> 0 us
  Pallas kernels: 54 us -> 53.1 us
    unnamed x24 -> x0, local copies, waits for them, and re-layouts: 7.61 us -> none
    pallas_call x1, Pallas kernels: 1.68 us -> 0.72 us  [fused(): pl.pallas_call(finish_kernel, grid=(1,), out_shape=tuple((jax.ShapeDtypeS...]
where the time goes in v2:
time: 54 us; the launch traced here: 53.8 us
  Pallas kernels  53.1 us (98%)
  between operations  0.64 us (1%)
    pallas_call x1, Pallas kernels, fused(): pl.pallas_call(functools.partial(cycle_kernel, g), out_shape=tuple((jax.S...  52.4 us

profile of v2, /device:TPU:0, one launch (start us, length us, event | category | flops | bytes accessed | tf_op | source)
XLA Modules:
  0.0 53.8 jit_solution(5390724438093030576)
XLA Ops:
  0.6 52.4 %shard_map.111 = (f32[256,128]{1,0:T(8,128)S(1)}, f32[256,128]{1,0:T(8,128)S(1)}, f32[64,128]{1,0:T(8,128)S(1)}, f32[8,128]{1,0:T(8,128)S(1)}) custom-call(bf16[2048,128]{1,0:T(8,128)(2,1)} %vals_h.1, bf16[2,2048]{1,0:T(2,128)(2,1)} %points0_h.1, bf16[2,512]{1,0:T(2,128)(2,1)} %points1_h.1, bf16[2,64]{1,0:T(2,128)(2,1)} %points2_h.1, ...), custom_call_target="tpu_custom_call" | custom-call | tf_op jit(solution)/shard_map/pallas_call | solution.py:552
  53.1 0.7 %shard_map.112 = (f32[256,128]{1,0:T(8,128)}, f32[256,128]{1,0:T(8,128)}, f32[64,128]{1,0:T(8,128)}, f32[1,1]{1,0:T(1,128)}) custom-call(f32[256,128]{1,0:T(8,128)S(1)} %get-tuple-element.12.fine, f32[256,128]{1,0:T(8,128)S(1)} %get-tuple-element.13.mid, f32[64,128]{1,0:T(8,128)S(1)} %get-tuple-element.14.coarse, f32[8,128]{1,0:T(8,128)S(1)} %get-tuple-element.15.norm), custom_call_target="tpu_custom_call" | custom-call | tf_op jit(solution)/shard_map/pallas_call | solution.py:561

commit v3 on v2

v3 whole, which is shorter than its diff:
```python
import functools
import math

import jax
import jax.numpy as jnp
from jax import lax
from jax.experimental import pallas as pl
from jax.experimental.pallas import tpu as pltpu
from jax.sharding import PartitionSpec as P

TILE = 128


support_fine = 0.35
support_mid = 0.55
support_coarse = 0.8


def spread(x, axis, root):
    mine = lax.axis_index(axis) == root
    return lax.psum(jnp.where(mine, x, jnp.zeros_like(x)), axis)


def wendland(left_pts, right_pts, support):
    left = left_pts.astype(jnp.float32)
    right = right_pts.astype(jnp.float32)
    across = left[0][..., :, None] - right[0][..., None, :]
    upward = left[1][..., :, None] - right[1][..., None, :]
    ratio_t = jnp.sqrt(across * across + upward * upward) / support
    margin = jnp.maximum(1.0 - ratio_t, 0.0)
    squared = margin * margin
    return (squared * squared * (4.0 * ratio_t + 1.0)).astype(jnp.bfloat16)


def listed_terms(row_pts, col_pts, listing, vector, support, flipped):
    row_tiles = row_pts.reshape(2, -1, TILE)
    col_tiles = col_pts.reshape(2, -1, TILE)
    listed = listing.shape[-1]
    group = math.gcd(listed, 32)
    order = listing.reshape(2, listed // group, group)
    fields = vector.shape[-1]
    inputs = vector.reshape(-1, TILE, fields)
    target = col_tiles.shape[1] if flipped else row_tiles.shape[1]
    total = jnp.zeros((target, TILE, fields), jnp.float32)

    def add_group(total, pair):
        tile_rows, tile_cols = pair
        kernel = wendland(row_tiles[:, tile_rows], col_tiles[:, tile_cols], support)
        if flipped:
            contrib = jnp.einsum(
                "gij,gir->gjr", kernel, inputs[tile_rows], preferred_element_type=jnp.float32
            )
            return (total.at[tile_cols].add(contrib), None)
        contrib = jnp.einsum(
            "gij,gjr->gir", kernel, inputs[tile_cols], preferred_element_type=jnp.float32
        )
        return (total.at[tile_rows].add(contrib), None)

    total, unused = lax.scan(add_group, total, (order[0], order[1]))
    return total.reshape(-1, fields)


def per_device(values, points0, points1, points2, tiles_a0, tiles_e1, tiles_a1, factor):
    row_count = lax.axis_size("row")
    col_count = lax.axis_size("col")
    col_id = lax.axis_index("col")
    col_per_row = col_count // row_count
    rows_fine, fields = values.shape
    rows_mid = points1.shape[1]
    share = rows_fine // col_count
    cols_fine = rows_fine // col_per_row
    cols_mid = rows_mid // col_per_row
    source = col_id // col_per_row
    part_index = col_id % col_per_row
    value_piece = lax.dynamic_slice_in_dim(values, part_index * cols_fine, cols_fine, 0)
    fine_piece = lax.dynamic_slice_in_dim(points0, part_index * cols_fine, cols_fine, 1)
    mid_piece = lax.dynamic_slice_in_dim(points1, part_index * cols_mid, cols_mid, 1)
    value_cols, fine_cols, mid_cols = (
        spread(value_piece, "row", source),
        spread(fine_piece, "row", source),
        spread(mid_piece, "row", source),
    )
    scale_a0 = (rows_fine / (col_count * tiles_a0.shape[-1] * TILE * TILE)) ** 0.5
    scale_e1 = (rows_fine / (col_count * tiles_e1.shape[-1] * TILE * TILE)) ** 0.5
    scale_a1 = (rows_mid / (col_count * tiles_a1.shape[-1] * TILE * TILE)) ** 0.5
    scale_e2 = (1.0 / (rows_mid * row_count)) ** 0.5
    fine_data = values.astype(jnp.float32)
    own_data = lax.dynamic_slice_in_dim(values, col_id * share, share, 0).astype(jnp.float32)
    product_part = listed_terms(points0, fine_cols, tiles_a0[0, 0], value_cols, support_fine, False)
    product_whole = lax.psum(product_part, "col")
    fine_residual = fine_data - 0.5 * (scale_a0 * product_whole)
    fine_square = jnp.sum(fine_residual * fine_residual)
    restrict_part = listed_terms(
        points0, mid_cols, tiles_e1[0, 0], fine_residual.astype(jnp.bfloat16), support_mid, True
    )
    restrict_sum = lax.psum(restrict_part, "row")
    mid_data = scale_e1 * restrict_sum
    mid_part = listed_terms(
        points1, mid_cols, tiles_a1[0, 0], mid_data.astype(jnp.bfloat16), support_mid, False
    )
    mid_whole = (scale_a1 * lax.psum(mid_part, "col")).astype(jnp.bfloat16)
    mid_slice = lax.dynamic_slice_in_dim(mid_whole, part_index * cols_mid, cols_mid, 0)
    mid_turned = spread(mid_slice, "row", source)
    mid_residual = mid_data - 0.5 * mid_turned.astype(jnp.float32)
    coarse_kernel = wendland(points2, mid_cols, support_coarse)
    coarse_part = jnp.dot(
        coarse_kernel, mid_residual.astype(jnp.bfloat16), preferred_element_type=jnp.float32
    )
    coarse_sum = lax.psum(coarse_part, "col")
    coarse_data = (scale_e2 * coarse_sum).astype(jnp.bfloat16)
    halfway_part = lax.dot_general(
        factor, coarse_data, (((0,), (0,)), ((), ())), preferred_element_type=jnp.float32
    )
    halfway = lax.psum(halfway_part, "row").astype(jnp.bfloat16)
    coarse_part_two = jnp.dot(factor, halfway, preferred_element_type=jnp.float32)
    coarse_coef = lax.psum(coarse_part_two, "col")
    prolong_part = lax.dot_general(
        coarse_kernel,
        coarse_coef.astype(jnp.bfloat16),
        (((0,), (0,)), ((), ())),
        preferred_element_type=jnp.float32,
    )
    mid_coef = 0.5 * mid_data + scale_e2 * lax.psum(prolong_part, "row")
    fine_part = listed_terms(
        points0, mid_cols, tiles_e1[0, 0], mid_coef.astype(jnp.bfloat16), support_mid, False
    )
    fine_coef = 0.5 * own_data + scale_e1 * lax.psum_scatter(
        fine_part, "col", scatter_dimension=0, tiled=True
    )
    fine_total = lax.psum(fine_square / col_count, ("row", "col"))
    fine_norm = fine_total / (rows_fine * row_count * fields)
    return (fine_coef, mid_coef, coarse_coef, jnp.stack([fine_norm]))


FAR = 64.0
MESH = pl.DeviceIdType.MESH


def phi_of(square, support):
    square = jnp.maximum(square, 1e-20)
    distance = square * lax.rsqrt(square)
    margin = jnp.maximum(support - distance, 0.0)
    squared = margin * margin
    return (squared * squared * (1.25 * support - margin)).astype(jnp.bfloat16)


def gain(support):
    return 4.0 / support ** 5


def dot(a, b):
    return jnp.dot(a, b, preferred_element_type=jnp.float32)


def far_rows(tiles, row_tiles, col_tiles, by_col):
    row, col = tiles[0, 0, 0:1, :], tiles[0, 0, 1:2, :]
    key = col * row_tiles + row if by_col else row * col_tiles + col
    count = row_tiles * col_tiles
    place = lax.broadcasted_iota(jnp.int32, (count, key.shape[1]), 0)
    near = jnp.max(jnp.where(place == key, 1.0, 0.0), axis=1, keepdims=True)
    return jnp.broadcast_to(FAR * (1.0 - near), (count, TILE))


def halves(x):
    high = x.astype(jnp.bfloat16)
    return high, (x - high.astype(jnp.float32)).astype(jnp.bfloat16)


def describe(ref, lanes, x, y):
    norm = x * x + y * y
    first = norm.astype(jnp.bfloat16).astype(jnp.float32)
    second = (norm - first).astype(jnp.bfloat16).astype(jnp.float32)
    for k, line in enumerate((-2.0 * x, -2.0 * y, first, second, norm - first - second)):
        ref[k:k + 1, lanes] = line


def flipped_side(sides):
    return jnp.concatenate([-0.5 * sides[0:2], sides[5:8], sides[2:5]], axis=0)


def cycle_kernel(g, vals_h, points0_h, points1_h, points2_h, tiles_a0_h, tiles_e1_h, tiles_a1_h, factor_h,
                 fine_o, mid_o, coarse_o, norm_o,
                 tiles_a0, tiles_e1, tiles_a1, factor, points2,
                 v2, p0g, p1g, pcg, maskg, emask, tmask, masks_s, emask_s, tmask_s, fac, facg, gtg,
                 gall, gmid, gcoarse, gfine, gplane, gmids, gcs, fbuf, side_a, side_e, side_t, side_o, side_m,
                 a0, e1own, e1t, e2t, a1t, other_s, other_r, resg, part_buf, rsin, mida, csend, crecv, cg, wcat, zcat,
                 l_s, a_m, p0_m, p1_m, pc_m, v_m, em_m, tm_m, f_m, g_m, ot_m, re_m, rs_m, mz_m, ma_m, cr_m, ca_m):
    nr, nc, R0, R1, R2 = g["nr"], g["nc"], g["R0"], g["R1"], g["R2"]
    D = nr * nc
    T0, T1 = R0 // TILE, R1 // TILE
    C0, C1 = R0 * nr // nc, R1 * nr // nc
    B0, B1 = C0 // TILE, C1 // TILE
    S0 = R0 // nc
    I0 = S0 // TILE
    Q1 = C1 // nr
    N1, N2 = nr * R1, g["N2"]
    CR = N2 // D
    NT1 = nr * T1
    NT2 = N2 // TILE
    f32, bf16 = jnp.float32, jnp.bfloat16
    r = lax.axis_index("row")
    c = lax.axis_index("col")
    d = r * nc + c
    y, k_core = r // 2, lax.rem(r, 2)
    z, h = c // 2, lax.rem(c, 2)
    mate = r + 1 - 2 * k_core
    yp = lax.rem(r + 2, nr)
    diag = lax.rem(mate + 2, nr)
    xp = c + 1 - 2 * h
    own_b = 2 * r + h

    def rc(src, dst, ssem, rsem, rr, cc):
        return pltpu.make_async_remote_copy(src_ref=src, dst_ref=dst, send_sem=ssem, recv_sem=rsem,
                                            device_id=(rr, cc), device_id_type=MESH)

    def each(lo, hi, f):
        def body(k, carry):
            f(k)
            return carry
        lax.fori_loop(lo, hi, body, 0)

    barrier = pltpu.get_barrier_semaphore()

    def greet(k):
        q = lax.rem(c + k, nc)
        for j in range(nr):
            pl.semaphore_signal(barrier, inc=1, device_id=(lax.rem(r + j, nr), q), device_id_type=MESH)

    each(1, nc, greet)
    for j in range(1, nr):
        pl.semaphore_signal(barrier, inc=1, device_id=(lax.rem(r + j, nr), c), device_id_type=MESH)
    loads = [pltpu.make_async_copy(s, t, l_s.at[k]) for k, (s, t) in enumerate((
        (points0_h, p0g.at[r]), (points1_h, p1g.at[r]), (points2_h, points2), (tiles_a0_h, tiles_a0),
        (tiles_e1_h, tiles_e1), (tiles_a1_h, tiles_a1), (factor_h, factor), (vals_h, v2.at[k_core])))]
    for load in loads:
        load.start()

    def one_hot(ref, rows, columns):
        ref[16:16 + rows] = jnp.where(lax.broadcasted_iota(jnp.int32, (rows, columns), 1) // TILE
                                      == lax.broadcasted_iota(jnp.int32, (rows, columns), 0), 1.0, 0.0).astype(bf16)

    one_hot(gfine, 2 * T0, 2 * R0)
    one_hot(gplane, T0, R0)
    one_hot(gmids, NT1, N1)
    fbuf[...] = jnp.zeros_like(fbuf)
    emask_s[...] = jnp.zeros_like(emask_s)
    tmask_s[...] = jnp.zeros_like(tmask_s)
    for ref in (gall, gmid, gcoarse):
        ref[...] = jnp.ones_like(ref)
    for load in loads[:-1]:
        load.wait()
    far_a0 = far_rows(tiles_a0, T0, B0, False)
    far_e1 = far_rows(tiles_e1, T0, B1, False)
    for q in range(nc):
        masks_s[q] = far_a0[q * I0 * B0:(q + 1) * I0 * B0].astype(bf16)
        emask_s[q, :I0 * B1] = far_e1[q * I0 * B1:(q + 1) * I0 * B1]
    far_e1 = far_rows(tiles_e1, T0, B1, True)
    far_a1 = far_rows(tiles_a1, T1, B1, True)
    planes = nc // 2
    PT = T0 // planes
    for q in range(planes):
        for j in range(B1):
            tmask_s[q, j * PT:(j + 1) * PT] = far_e1[j * T0 + q * PT:j * T0 + (q + 1) * PT]
        j = q * Q1 // TILE
        tmask_s[q, B1 * PT:B1 * PT + T1] = far_a1[j * T1:(j + 1) * T1]
    half_of = lax.rem(r, TILE // R2)
    raw = factor[...].astype(f32)
    fac[...] = jnp.concatenate([jnp.where(half_of == k, raw, 0.0) for k in range(TILE // R2)], axis=1).astype(bf16)
    line = points2[...].astype(f32)
    pcg[r] = jnp.zeros((8, TILE), f32)
    pcg[r, 0:2] = jnp.concatenate([jnp.where(half_of == k, line, 0.0) for k in range(TILE // R2)], axis=1)
    loads[-1].wait()
    pl.semaphore_wait(barrier, D - 1)

    def row_send(src, dst, m):
        for k in range(1, nr):
            rc(src, dst, m.at[0], m.at[1], lax.rem(r + k, nr), c).start()

    def row_wait(ref, m):
        slots = ref.at[pl.ds(0, nr - 1)]
        rc(slots, slots, m.at[0], m.at[1], mate, c).wait()

    def col_send(src_of, dst, m):
        def go(k):
            q = lax.rem(c + k, nc)
            rc(src_of(q), dst, m.at[0], m.at[1], r, q).start()
        each(1, nc, go)

    y_of = c // planes
    mask_row = 2 * y_of + k_core
    mask_slot = jnp.where(y_of == y, 0, 1) * planes + lax.rem(c, planes)
    mask_self = y_of == y

    def mask_go(k):
        q = lax.rem(c + k, nc)
        rc(masks_s.at[q], maskg.at[mask_slot], a_m.at[0], a_m.at[1], mask_row, q).start()

    each(1, nc, mask_go)

    @pl.when(jnp.logical_not(mask_self))
    def _():
        mask_go(0)

    @pl.when(mask_self)
    def _():
        maskg[mask_slot] = masks_s[c]

    row_send(p0g.at[r], p0g.at[r], p0_m)
    rc(v2.at[k_core], v2.at[k_core], v_m.at[0], v_m.at[1], mate, c).start()
    row_send(p1g.at[r], p1g.at[r], p1_m)
    row_send(pcg.at[r], pcg.at[r], pc_m)
    tmask_self = c // 2 == r

    def tmask_go(q):
        rc(tmask_s.at[q], tmask.at[r], tm_m.at[0], tm_m.at[1], c // 2, 2 * q + h).start()

    for k in range(1, planes):
        tmask_go(lax.rem(z + k, planes))

    @pl.when(jnp.logical_not(tmask_self))
    def _():
        tmask_go(z)

    @pl.when(tmask_self)
    def _():
        tmask[r] = tmask_s[z]

    col_send(lambda q: emask_s.at[q], emask.at[c], em_m)
    row_send(fac, facg.at[r], f_m)
    emask[c] = emask_s[c]
    facg[r] = fac[...]

    def describe_fine(rb):
        describe(gall.at[rb], slice(None), p0g[rb, 0:1, :].astype(f32), p0g[rb, 1:2, :].astype(f32))

    describe_fine(r)
    row_wait(p0g, p0_m)
    for rb in (mate, yp, diag):
        describe_fine(rb)
    for k in range(2):
        gfine[:16, k * R0:(k + 1) * R0] = jnp.concatenate(
            [gall[2 * y + k], jnp.zeros((8, R0), f32)], axis=0).astype(bf16)
    row_wait(p1g, p1_m)
    for q in range(nr):
        describe(gmid, slice(q * R1, (q + 1) * R1), p1g[q, 0:1, :].astype(f32), p1g[q, 1:2, :].astype(f32))
    gmids[:16] = jnp.concatenate([gmid[...], jnp.zeros((8, N1), f32)], axis=0).astype(bf16)
    strip = pl.ds(pl.multiple_of(c * S0, S0), S0)
    for s, rb in enumerate((r, yp)):
        fbuf[0:8, s * S0:(s + 1) * S0] = flipped_side(gall[rb, :, strip])

    def wait_slots(ref, n, m):
        slots = ref.at[pl.ds(0, n)]
        rc(slots, slots, m.at[0], m.at[1], mate, c).wait()

    @pl.when(mask_self)
    def _():
        wait_slots(maskg, nc - 1, a_m)

    @pl.when(jnp.logical_not(mask_self))
    def _():
        wait_slots(maskg, nc, a_m)

    for s in range(2):
        for q in range(planes):
            rows = maskg[s * planes + q].astype(f32)
            for i in range(I0):
                fbuf[16 + q * B0:16 + (q + 1) * B0, (s * I0 + i) * TILE:(s * I0 + i + 1) * TILE] = rows[i * B0:(i + 1) * B0]
    side_a[...] = fbuf[...].T.astype(bf16)

    def build(put, side, sides, depth, support, columns, step):
        def go(k):
            lanes = pl.ds(pl.multiple_of(k * step, step), step)
            put(lanes, phi_of(dot(side[:, :depth], sides[:depth, lanes]), support))
        each(0, columns // step, go)

    def put_a0(s):
        def put(lanes, value):
            a0[s, :, lanes] = value
        return put

    KA = 16 + 2 * T0
    build(put_a0(1), side_a.at[pl.ds(S0, S0)], gfine, KA, support_fine, 2 * R0, 512)
    rc(v2.at[1 - k_core], v2.at[1 - k_core], v_m.at[0], v_m.at[1], mate, c).wait()
    other_s[...] = (dot(a0[1, :, :R0], v2[0]) + dot(a0[1, :, R0:], v2[1])).astype(bf16)
    rc(other_s, other_r, ot_m.at[0], ot_m.at[1], yp, c).start()
    build(put_a0(0), side_a.at[pl.ds(0, S0)], gfine, KA, support_fine, 2 * R0, 512)
    acc = dot(a0[0, :, :R0], v2[0]) + dot(a0[0, :, R0:], v2[1])
    own_vals = v2[k_core, strip, :].astype(f32)
    rc(other_s, other_r, ot_m.at[0], ot_m.at[1], yp, c).wait()
    res = own_vals - (0.5 * g["scale_a0"] * gain(support_fine)) * (acc + other_r[...].astype(f32))
    resg[own_b] = res.astype(bf16).reshape(2, S0 // 2, -1)

    def plane_gather(ref, m, depth):
        first, second = pl.ds(0, depth // 2), pl.ds(depth // 2, depth // 2)
        x_slot, y_slot, d_slot = 2 * r + 1 - h, 2 * yp + h, 2 * yp + 1 - h

        def send(part, sem, rr, cc):
            rc(part, part, m.at[0], m.at[sem], rr, cc).start()

        def take(part, sem):
            rc(part, part, m.at[0], m.at[sem], mate, c).wait_recv()

        def start():
            send(ref.at[own_b], 1, r, xp)
            send(ref.at[own_b], 2, yp, c)
            send(ref.at[own_b], 5, mate, c)

        def pass_x():
            take(ref.at[x_slot], 1)
            send(ref.at[x_slot, first], 3, yp, c)
            send(ref.at[x_slot], 5, mate, c)

        def pass_y():
            take(ref.at[y_slot], 2)
            send(ref.at[y_slot, second], 4, r, xp)
            send(ref.at[y_slot], 5, mate, c)

        def pass_d():
            take(ref.at[d_slot, first], 3)
            send(ref.at[d_slot, first], 5, mate, c)
            take(ref.at[d_slot, second], 4)
            send(ref.at[d_slot, second], 5, mate, c)

        def end():
            take(ref.at[pl.ds(0, 4)], 5)

        def drain():
            part = ref.at[pl.ds(0, 7)]
            rc(part, part, m.at[0], m.at[5], mate, c).wait_send()
        return start, pass_x, pass_y, pass_d, end, drain

    res_start, res_x, res_y, res_d, res_end, res_drain = plane_gather(resg, re_m, 2)
    res_start()
    for q in range(nr):
        gplane[:16, q * PT * TILE:(q + 1) * PT * TILE] = jnp.concatenate(
            [gall[q, :, pl.ds(pl.multiple_of(z * PT * TILE, PT * TILE), PT * TILE)],
             jnp.zeros((8, PT * TILE), f32)], axis=0).astype(bf16)

    @pl.when(tmask_self)
    def _():
        wait_slots(tmask, nr - 1, tm_m)

    @pl.when(jnp.logical_not(tmask_self))
    def _():
        wait_slots(tmask, nr, tm_m)

    block = pl.ds(pl.multiple_of(own_b * C1, C1), C1)
    fbuf[0:8, :C1] = flipped_side(gmid[:, block])
    for q in range(nr):
        for j in range(B1):
            fbuf[16 + q * PT:16 + (q + 1) * PT, j * TILE:(j + 1) * TILE] = tmask[q, j * PT:(j + 1) * PT, :]
    own_tile = pl.ds(pl.multiple_of(own_b * C1 + (z * Q1) // TILE * TILE, TILE), TILE)
    fbuf[0:8, C1:C1 + TILE] = flipped_side(gmid[:, own_tile])
    for q in range(nr):
        fbuf[16 + q * T1:16 + (q + 1) * T1, C1:C1 + TILE] = tmask[q, B1 * PT:B1 * PT + T1, :]
    side_t[...] = fbuf[...].T.astype(bf16)

    def put_e1t(lanes, value):
        e1t[:, lanes] = value

    build(put_e1t, side_t.at[pl.ds(0, C1)], gplane, 16 + T0, support_mid, R0, 512)
    row_wait(pcg, pc_m)
    row_wait(facg, f_m)
    res_x()
    res_y()
    strips = []
    per = TILE // R2
    for lane in range(NT2):
        total = facg[lane * per].astype(f32)
        for k in range(1, per):
            total = total + facg[lane * per + k].astype(f32)
        strips.append(total)
    gtg[c] = jnp.concatenate(strips, axis=1).astype(bf16)
    col_send(lambda q: gtg.at[c], gtg.at[c], g_m)
    for t in range(NT2):
        line = pcg[per * t] + pcg[per * t + 1]
        describe(gcoarse, slice(t * TILE, (t + 1) * TILE), line[0:1], line[1:2])
    gcs[...] = jnp.concatenate([gcoarse[...], jnp.zeros((8, N2), f32)], axis=0).astype(bf16)
    wide = fbuf.shape[1]
    for q in range(N1 // wide):
        fbuf[0:8] = flipped_side(gmid[:, q * wide:(q + 1) * wide])
        side_m[...] = fbuf[...].T.astype(bf16)
        e2t[q * wide:(q + 1) * wide] = phi_of(dot(side_m[:, :16], gcs[...]), support_coarse)
    res_d()

    def put_a1t(lanes, value):
        a1t[:, lanes] = value

    own_half = pl.ds(pl.multiple_of(C1 + lax.rem(z * Q1, TILE), Q1), Q1)
    build(put_a1t, side_t.at[own_half], gmids, 16 + NT1, support_mid, N1, 1024)
    own_mids = pl.ds(pl.multiple_of(own_b * C1 + z * Q1, Q1), Q1)
    coarse_gain = g["scale_e2"] * gain(support_coarse)
    turned_w = coarse_gain * (e2t[own_mids, :].astype(f32)
                              - (0.5 * g["scale_a1"] * gain(support_mid)) * dot(a1t[...], e2t[...]))
    w_high, w_low = halves(turned_w)
    w_pair = jnp.concatenate([w_high.astype(f32), w_low.astype(f32)], axis=0).T.astype(bf16)
    wcat[:, :TILE] = w_pair
    wcat[:, TILE:] = w_pair
    res_end()
    plane = resg[...].reshape(R0, -1)
    restricted = dot(e1t[...], plane)
    held = plane.astype(f32)
    square = jnp.sum((held * held).reshape(R0 // 16, 16, -1), axis=0)
    for q in range(planes):
        part_buf[q] = jnp.concatenate([restricted[q * Q1:(q + 1) * Q1], square], axis=0).astype(bf16)

    def z_send(src_of, dst, m):
        for k in range(1, planes):
            q = lax.rem(z + k, planes)
            rc(src_of(q), dst, m.at[0], m.at[1], r, 2 * q + h).start()

    z_send(lambda q: part_buf.at[q], rsin.at[z], rs_m)
    rsin[z] = part_buf[z]
    wait_slots(emask, nc - 1, em_m)
    fbuf[0:8, :S0] = flipped_side(gall[r, :, strip])
    for q in range(nc):
        for i in range(I0):
            fbuf[16 + q * B1:16 + (q + 1) * B1, i * TILE:(i + 1) * TILE] = emask[q, i * B1:(i + 1) * B1, :]
    side_e[...] = fbuf[:, :S0].T.astype(bf16)

    def put_e1own(lanes, value):
        e1own[:, lanes] = value

    build(put_e1own, side_e, gmids, 16 + NT1, support_mid, N1, 512)
    wait_slots(gtg, nc - 1, g_m)
    gt = gtg[...].reshape(N2, N2)
    gg_high, gg_low = halves(dot(gt.astype(f32).T.astype(bf16), gt))
    zcat[S0 + C1:, :N2] = gg_high
    zcat[S0 + C1:, N2:] = gg_low
    fine_gain = g["scale_e1"] * gain(support_mid)
    h_high, h_low = halves((fine_gain * coarse_gain) * dot(e1own[...], e2t[...]))
    steps = (dot(h_high, gg_high) + dot(h_low, gg_high) + dot(h_high, gg_low),)
    rows_c = e2t[pl.ds(pl.multiple_of(c * C1, C1), C1), :]
    steps += (coarse_gain * (dot(rows_c, gg_high) + dot(rows_c, gg_low)),)
    for k, step in enumerate(steps):
        high, low = halves(step)
        zcat[k * C1:(k + 1) * C1, :N2] = high
        zcat[k * C1:(k + 1) * C1, N2:] = low

    wait_slots(rsin, planes - 1, rs_m)
    total = rsin[0].astype(f32)
    for q in range(1, planes):
        total = total + rsin[q].astype(f32)
    q_high, q_low = halves(fine_gain * total[:Q1])
    part = dot(wcat[...], jnp.concatenate([q_high, q_high, q_low, q_low], axis=0))
    csend[...] = part.reshape(D, CR, -1).astype(bf16)

    def all_send(src_of, dst, m):
        def go(k):
            q = lax.rem(c + k, nc)
            for j in range(nr):
                p = lax.rem(r + j, nr)
                rc(src_of(p * nc + q), dst, m.at[0], m.at[1], p, q).start()
        each(1, nc, go)
        for j in range(1, nr):
            p = lax.rem(r + j, nr)
            rc(src_of(p * nc + c), dst, m.at[0], m.at[1], p, c).start()

    all_send(lambda q: csend.at[q], crecv.at[d], cr_m)
    mida[own_b, z] = q_high
    z_send(lambda q: mida.at[own_b, z], mida.at[own_b, z], mz_m)
    crecv[d] = csend[d]
    norm_o[...] = jnp.broadcast_to(jnp.sum(total[Q1:], keepdims=True) * g["norm_scale"], norm_o.shape)
    wait_slots(crecv, D - 1, cr_m)
    cg[d] = jnp.sum(crecv[...].astype(f32), axis=0).astype(bf16)
    all_send(lambda q: cg.at[d], cg.at[d], ca_m)
    mid_start, mid_x, mid_y, mid_d, mid_end, mid_drain = plane_gather(mida, ma_m, planes)
    arrived = mida.at[own_b, pl.ds(0, planes - 1)]
    rc(arrived, arrived, mz_m.at[0], mz_m.at[1], mate, c).wait()
    mid_start()
    mid_x()
    mid_y()
    wait_slots(cg, D - 1, ca_m)
    cd = cg[...].astype(f32).reshape(N2, -1).astype(bf16)
    both = jnp.concatenate([cd, cd], axis=0)
    coarse_o[...] = dot(zcat[pl.ds(pl.multiple_of(S0 + C1 + r * R2, R2), R2), :], both)
    mid_d()
    mid_end()
    mid_o[...] = 0.5 * mida[c].astype(f32).reshape(C1, -1) + dot(zcat[S0:S0 + C1, :], both)
    fine_o[...] = (0.5 * own_vals + (0.5 * fine_gain) * dot(e1own[...], mida[...].reshape(N1, -1))
                   + dot(zcat[:S0, :], both))
    res_drain()
    mid_drain()


def finish_kernel(fine, mid, coarse, norm, fine_o, mid_o, coarse_o, norm_o):
    fine_o[...] = fine[...]
    mid_o[...] = mid[...]
    coarse_o[...] = coarse[...]
    norm_o[...] = norm[0:1, 0:1]


def fits(nr, nc, R0, R1, R2):
    if nr != 4 or nc != 8:
        return False
    if R0 != R1 * nr or R0 != 2 * nc * TILE or 2 * R2 != TILE:
        return False
    return True


def fused(values, points0, points1, points2, tiles_a0, tiles_e1, tiles_a1, factor):
    nr, nc = lax.axis_size("row"), lax.axis_size("col")
    R0, R1, R2 = points0.shape[1], points1.shape[1], points2.shape[1]
    F = values.shape[-1]
    if not fits(nr, nc, R0, R1, R2) or F != TILE:
        return per_device(values, points0, points1, points2, tiles_a0, tiles_e1, tiles_a1, factor)
    D, N2 = nr * nc, nr * R2
    T0, T1 = R0 // TILE, R1 // TILE
    B0, B1 = R0 * nr // nc // TILE, R1 * nr // nc // TILE
    S0 = R0 // nc
    I0 = S0 // TILE
    C1, CR, Q1 = B1 * TILE, N2 // D, R1 * nr // nc // nr
    g = dict(nr=nr, nc=nc, R0=R0, R1=R1, R2=R2, N2=N2,
             scale_a0=(R0 / (nc * tiles_a0.shape[-1] * TILE * TILE)) ** 0.5,
             scale_e1=(R0 / (nc * tiles_e1.shape[-1] * TILE * TILE)) ** 0.5,
             scale_a1=(R1 / (nc * tiles_a1.shape[-1] * TILE * TILE)) ** 0.5,
             scale_e2=(1.0 / (R1 * nr)) ** 0.5,
             norm_scale=1.0 / (R0 * nr * F))
    f32, bf16, i32 = jnp.float32, jnp.bfloat16, jnp.int32
    V = pltpu.VMEM
    dma = pltpu.SemaphoreType.DMA
    wide = N2 // nc
    N1 = nr * R1
    planes = nc // 2
    scratch = [
        V(tiles_a0.shape, i32), V(tiles_e1.shape, i32), V(tiles_a1.shape, i32), V((wide, R2), bf16), V(points2.shape, bf16),
        V((2, R0, F), bf16), V((nr,) + points0.shape, bf16), V((nr,) + points1.shape, bf16), V((nr, 8, TILE), f32),
        V((nc, I0 * B0, TILE), bf16), V((nc, 8, TILE), f32), V((nr, 16, TILE), f32),
        V((nc, I0 * B0, TILE), bf16), V((nc, 8, TILE), f32), V((planes, 16, TILE), f32),
        V((wide, TILE), bf16), V((nr, wide, TILE), bf16), V((nc, wide, N2), bf16),
        V((nr, 8, R0), f32), V((8, N1), f32), V((8, N2), f32),
        V((16 + 2 * T0, 2 * R0), bf16), V((16 + T0, R0), bf16), V((16 + nr * T1, N1), bf16), V((16, N2), bf16),
        V((TILE, 2 * S0), f32), V((2 * S0, TILE), bf16), V((S0, TILE), bf16), V((2 * S0, TILE), bf16),
        V((8, TILE), bf16), V((2 * S0, TILE), bf16),
        V((2, S0, 2 * R0), bf16), V((S0, N1), bf16), V((C1, R0), bf16), V((N1, N2), bf16), V((Q1, N1), bf16),
        V((S0, F), bf16), V((S0, F), bf16), V((nc, 2, S0 // 2, F), bf16),
        V((planes, Q1 + 16, F), bf16), V((planes, Q1 + 16, F), bf16), V((nc, planes, Q1, F), bf16),
        V((D, CR, F), bf16), V((D, CR, F), bf16), V((D, CR, F), bf16), V((N2, 4 * Q1), bf16),
        V((S0 + C1 + N2, 2 * N2), bf16),
    ]
    for n in (8, 2, 2, 2, 2, 2, 2, 2, 2, 2, 2, 6, 2, 2, 6, 2, 2):
        scratch += [dma((n,))]
    vm = pl.BlockSpec(memory_space=pltpu.VMEM)
    shapes = ((S0, F), (C1, F), (R2, F))
    parts = pl.pallas_call(
        functools.partial(cycle_kernel, g),
        out_shape=tuple(jax.ShapeDtypeStruct(s, f32) for s in shapes + ((8, TILE),)),
        in_specs=[pl.BlockSpec(memory_space=pltpu.HBM)] * 8,
        out_specs=[vm] * 4,
        scratch_shapes=scratch,
        compiler_params=pltpu.CompilerParams(collective_id=0, has_side_effects=True, vmem_limit_bytes=48 << 20),
    )(*[pltpu.with_memory_space_constraint(x, pltpu.HBM) for x in (
        values, points0, points1, points2, tiles_a0, tiles_e1, tiles_a1, factor.T)])
    fine, mid, coarse, norm = pl.pallas_call(
        finish_kernel,
        grid=(1,),
        out_shape=tuple(jax.ShapeDtypeStruct(s, f32) for s in shapes + ((1, 1),)),
        in_specs=[vm] * 4,
        out_specs=[pl.BlockSpec(s, lambda i: (0, 0)) for s in shapes + ((1, 1),)],
        compiler_params=pltpu.CompilerParams(vmem_limit_bytes=4 << 20),
    )(*parts)
    return (fine, mid, coarse, norm.reshape(1))


def solution(mesh):
    return jax.shard_map(
        fused,
        mesh=mesh,
        in_specs=(
            P("row", None),
            P(None, "row"),
            P(None, "row"),
            P(None, "row"),
            P("row", "col", None, None),
            P("row", "col", None, None),
            P("row", "col", None, None),
            P("row", "col"),
        ),
        out_specs=(P(("row", "col"), None), P("col", None), P("row", None), P()),
        check_vma=False,
    )
```

time: 54 us -> 44.8 us (0.83)
  Pallas kernels: 53.1 us -> 43.6 us
    pallas_call x1, Pallas kernels: 52.4 us -> 42.8 us  [fused(): pl.pallas_call(functools.partial(cycle_kernel, g), out_shape=tuple((jax.S...]
where the time goes in v3:
time: 44.8 us; the launch traced here: 44.2 us
  Pallas kernels  43.6 us (97%)
  between operations  0.64 us (1%)
    pallas_call x1, Pallas kernels, fused(): pl.pallas_call(functools.partial(cycle_kernel, g), out_shape=tuple((jax.S...  42.8 us

profile of v3, /device:TPU:0, one launch (start us, length us, event | category | flops | bytes accessed | tf_op | source)
XLA Modules:
  0.0 44.2 jit_solution(7198501748587310487)
XLA Ops:
  0.6 42.8 %shard_map.111 = (f32[256,128]{1,0:T(8,128)S(1)}, f32[256,128]{1,0:T(8,128)S(1)}, f32[64,128]{1,0:T(8,128)S(1)}, f32[8,128]{1,0:T(8,128)S(1)}) custom-call(bf16[2048,128]{1,0:T(8,128)(2,1)} %vals_h.1, bf16[2,2048]{1,0:T(2,128)(2,1)} %points0_h.1, bf16[2,512]{1,0:T(2,128)(2,1)} %points1_h.1, bf16[2,64]{1,0:T(2,128)(2,1)} %points2_h.1, ...), custom_call_target="tpu_custom_call" | custom-call | tf_op jit(solution)/shard_map/pallas_call | solution.py:645
  43.5 0.7 %shard_map.112 = (f32[256,128]{1,0:T(8,128)}, f32[256,128]{1,0:T(8,128)}, f32[64,128]{1,0:T(8,128)}, f32[1,1]{1,0:T(1,128)}) custom-call(f32[256,128]{1,0:T(8,128)S(1)} %get-tuple-element.12.fine, f32[256,128]{1,0:T(8,128)S(1)} %get-tuple-element.13.mid, f32[64,128]{1,0:T(8,128)S(1)} %get-tuple-element.14.coarse, f32[8,128]{1,0:T(8,128)S(1)} %get-tuple-element.15.norm), custom_call_target="tpu_custom_call" | custom-call | tf_op jit(solution)/shard_map/pallas_call | solution.py:654

commit v4 on v3

--- a/solution.py
+++ b/solution.py
@@ -136,16 +136,14 @@
 MESH = pl.DeviceIdType.MESH
 
 
-def phi_of(square, support):
+EDGE = 4.0 ** 0.2
+
+
+def phi_of(square):
     square = jnp.maximum(square, 1e-20)
-    distance = square * lax.rsqrt(square)
-    margin = jnp.maximum(support - distance, 0.0)
+    margin = jnp.maximum(EDGE - square * lax.rsqrt(square), 0.0)
     squared = margin * margin
-    return (squared * squared * (1.25 * support - margin)).astype(jnp.bfloat16)
-
-
-def gain(support):
-    return 4.0 / support ** 5
+    return (squared * squared * (1.25 * EDGE - margin)).astype(jnp.bfloat16)
 
 
 def dot(a, b):
@@ -166,23 +164,32 @@
     return high, (x - high.astype(jnp.float32)).astype(jnp.bfloat16)
 
 
-def describe(ref, lanes, x, y):
-    norm = x * x + y * y
-    first = norm.astype(jnp.bfloat16).astype(jnp.float32)
-    second = (norm - first).astype(jnp.bfloat16).astype(jnp.float32)
-    for k, line in enumerate((-2.0 * x, -2.0 * y, first, second, norm - first - second)):
+def pieces(x):
+    first = x.astype(jnp.bfloat16).astype(jnp.float32)
+    second = (x - first).astype(jnp.bfloat16).astype(jnp.float32)
+    return first, second, x - first - second
+
+
+def describe(ref, lanes, x, y, support):
+    square = (EDGE / support) ** 2
+    lines = pieces(-2.0 * square * x) + pieces(-2.0 * square * y) + pieces(square * (x * x + y * y))
+    for k, line in enumerate(lines):
         ref[k:k + 1, lanes] = line
+    ref[12:13, lanes] = x
+    ref[13:14, lanes] = y
 
 
 def flipped_side(sides):
-    return jnp.concatenate([-0.5 * sides[0:2], sides[5:8], sides[2:5]], axis=0)
+    x, y = sides[12:13], sides[13:14]
+    one = jnp.ones_like(x)
+    return jnp.concatenate([x, x, x, y, y, y, one, one, one, sides[6:9], jnp.zeros((4, x.shape[1]), jnp.float32)], axis=0)
 
 
 def cycle_kernel(g, vals_h, points0_h, points1_h, points2_h, tiles_a0_h, tiles_e1_h, tiles_a1_h, factor_h,
                  fine_o, mid_o, coarse_o, norm_o,
                  tiles_a0, tiles_e1, tiles_a1, factor, points2,
                  v2, p0g, p1g, pcg, maskg, emask, tmask, masks_s, emask_s, tmask_s, fac, facg, gtg,
-                 gall, gmid, gcoarse, gfine, gplane, gmids, gcs, fbuf, side_a, side_e, side_t, side_o, side_m,
+                 gall, gstrip, gpl, gmid, gmid2, gcoarse, gfine, gplane, gmids, gcs, fbuf, side_a, side_e, side_t, side_o, side_m,
                  a0, e1own, e1t, e2t, a1t, other_s, other_r, resg, part_buf, rsin, mida, csend, crecv, cg, wcat, zcat,
                  l_s, a_m, p0_m, p1_m, pc_m, v_m, em_m, tm_m, f_m, g_m, ot_m, re_m, rs_m, mz_m, ma_m, cr_m, ca_m):
     nr, nc, R0, R1, R2 = g["nr"], g["nc"], g["R0"], g["R1"], g["R2"]
@@ -245,7 +252,7 @@
     fbuf[...] = jnp.zeros_like(fbuf)
     emask_s[...] = jnp.zeros_like(emask_s)
     tmask_s[...] = jnp.zeros_like(tmask_s)
-    for ref in (gall, gmid, gcoarse):
+    for ref in (gall, gstrip, gpl, gmid, gmid2, gcoarse):
         ref[...] = jnp.ones_like(ref)
     for load in loads[:-1]:
         load.wait()
@@ -261,8 +268,7 @@
     for q in range(planes):
         for j in range(B1):
             tmask_s[q, j * PT:(j + 1) * PT] = far_e1[j * T0 + q * PT:j * T0 + (q + 1) * PT]
-        j = q * Q1 // TILE
-        tmask_s[q, B1 * PT:B1 * PT + T1] = far_a1[j * T1:(j + 1) * T1]
+        tmask_s[q, B1 * PT:B1 * PT + B1 * T1] = far_a1
     half_of = lax.rem(r, TILE // R2)
     raw = factor[...].astype(f32)
     fac[...] = jnp.concatenate([jnp.where(half_of == k, raw, 0.0) for k in range(TILE // R2)], axis=1).astype(bf16)
@@ -330,23 +336,20 @@
     emask[c] = emask_s[c]
     facg[r] = fac[...]
 
-    def describe_fine(rb):
-        describe(gall.at[rb], slice(None), p0g[rb, 0:1, :].astype(f32), p0g[rb, 1:2, :].astype(f32))
-
-    describe_fine(r)
+    def line_of(ref, q, way, lanes=slice(None)):
+        return ref[q, way:way + 1, lanes].astype(f32)
+
+    def describe_own(rb, slot):
+        describe(gall.at[slot], slice(None), line_of(p0g, rb, 0), line_of(p0g, rb, 1), support_fine)
+        gfine[:16, pl.ds(pl.multiple_of(slot * R0, R0), R0)] = gall[slot].astype(bf16)
+
+    strip = pl.ds(pl.multiple_of(c * S0, S0), S0)
+    describe_own(r, k_core)
     row_wait(p0g, p0_m)
-    for rb in (mate, yp, diag):
-        describe_fine(rb)
-    for k in range(2):
-        gfine[:16, k * R0:(k + 1) * R0] = jnp.concatenate(
-            [gall[2 * y + k], jnp.zeros((8, R0), f32)], axis=0).astype(bf16)
-    row_wait(p1g, p1_m)
-    for q in range(nr):
-        describe(gmid, slice(q * R1, (q + 1) * R1), p1g[q, 0:1, :].astype(f32), p1g[q, 1:2, :].astype(f32))
-    gmids[:16] = jnp.concatenate([gmid[...], jnp.zeros((8, N1), f32)], axis=0).astype(bf16)
-    strip = pl.ds(pl.multiple_of(c * S0, S0), S0)
-    for s, rb in enumerate((r, yp)):
-        fbuf[0:8, s * S0:(s + 1) * S0] = flipped_side(gall[rb, :, strip])
+    describe_own(mate, 1 - k_core)
+    describe(gstrip, slice(None), line_of(p0g, yp, 0, strip), line_of(p0g, yp, 1, strip), support_fine)
+    fbuf[0:16, :S0] = flipped_side(gall[k_core, :, strip])
+    fbuf[0:16, S0:] = flipped_side(gstrip[...])
 
     def wait_slots(ref, n, m):
         slots = ref.at[pl.ds(0, n)]
@@ -367,10 +370,10 @@
                 fbuf[16 + q * B0:16 + (q + 1) * B0, (s * I0 + i) * TILE:(s * I0 + i + 1) * TILE] = rows[i * B0:(i + 1) * B0]
     side_a[...] = fbuf[...].T.astype(bf16)
 
-    def build(put, side, sides, depth, support, columns, step):
+    def build(put, side, sides, depth, columns, step):
         def go(k):
             lanes = pl.ds(pl.multiple_of(k * step, step), step)
-            put(lanes, phi_of(dot(side[:, :depth], sides[:depth, lanes]), support))
+            put(lanes, phi_of(dot(side[:, :depth], sides[:depth, lanes])))
         each(0, columns // step, go)
 
     def put_a0(s):
@@ -379,62 +382,54 @@
         return put
 
     KA = 16 + 2 * T0
-    build(put_a0(1), side_a.at[pl.ds(S0, S0)], gfine, KA, support_fine, 2 * R0, 512)
+    build(put_a0(1), side_a.at[pl.ds(S0, S0)], gfine, KA, 2 * R0, 2048)
     rc(v2.at[1 - k_core], v2.at[1 - k_core], v_m.at[0], v_m.at[1], mate, c).wait()
     other_s[...] = (dot(a0[1, :, :R0], v2[0]) + dot(a0[1, :, R0:], v2[1])).astype(bf16)
     rc(other_s, other_r, ot_m.at[0], ot_m.at[1], yp, c).start()
-    build(put_a0(0), side_a.at[pl.ds(0, S0)], gfine, KA, support_fine, 2 * R0, 512)
+    build(put_a0(0), side_a.at[pl.ds(0, S0)], gfine, KA, 2 * R0, 2048)
     acc = dot(a0[0, :, :R0], v2[0]) + dot(a0[0, :, R0:], v2[1])
     own_vals = v2[k_core, strip, :].astype(f32)
     rc(other_s, other_r, ot_m.at[0], ot_m.at[1], yp, c).wait()
-    res = own_vals - (0.5 * g["scale_a0"] * gain(support_fine)) * (acc + other_r[...].astype(f32))
-    resg[own_b] = res.astype(bf16).reshape(2, S0 // 2, -1)
-
-    def plane_gather(ref, m, depth):
-        first, second = pl.ds(0, depth // 2), pl.ds(depth // 2, depth // 2)
-        x_slot, y_slot, d_slot = 2 * r + 1 - h, 2 * yp + h, 2 * yp + 1 - h
-
-        def send(part, sem, rr, cc):
-            rc(part, part, m.at[0], m.at[sem], rr, cc).start()
-
-        def take(part, sem):
-            rc(part, part, m.at[0], m.at[sem], mate, c).wait_recv()
+    res = own_vals - (0.5 * g["scale_a0"]) * (acc + other_r[...].astype(f32))
+    resg[own_b] = res.astype(bf16)
+
+    x_slot, y_slot, d_slot = 2 * r + 1 - h, 2 * yp + h, 2 * diag + 1 - h
+
+    def plane_gather(ref, m):
+        def send(slot, sem, rr, cc):
+            rc(ref.at[slot], ref.at[slot], m.at[0], m.at[sem], rr, cc).start()
 
         def start():
-            send(ref.at[own_b], 1, r, xp)
-            send(ref.at[own_b], 2, yp, c)
-            send(ref.at[own_b], 5, mate, c)
-
-        def pass_x():
-            take(ref.at[x_slot], 1)
-            send(ref.at[x_slot, first], 3, yp, c)
-            send(ref.at[x_slot], 5, mate, c)
-
-        def pass_y():
-            take(ref.at[y_slot], 2)
-            send(ref.at[y_slot, second], 4, r, xp)
-            send(ref.at[y_slot], 5, mate, c)
-
-        def pass_d():
-            take(ref.at[d_slot, first], 3)
-            send(ref.at[d_slot, first], 5, mate, c)
-            take(ref.at[d_slot, second], 4)
-            send(ref.at[d_slot, second], 5, mate, c)
+            send(own_b, 1, r, xp)
+            send(own_b, 2, yp, c)
+            send(own_b, 3, diag, xp)
+            send(own_b, 4, mate, c)
+
+        def relay(slot, sem):
+            rc(ref.at[slot], ref.at[slot], m.at[0], m.at[sem], mate, c).wait_recv()
+            send(slot, 4, mate, c)
 
         def end():
-            take(ref.at[pl.ds(0, 4)], 5)
+            part = ref.at[pl.ds(0, 4)]
+            rc(part, part, m.at[0], m.at[4], mate, c).wait_recv()
 
         def drain():
             part = ref.at[pl.ds(0, 7)]
-            rc(part, part, m.at[0], m.at[5], mate, c).wait_send()
-        return start, pass_x, pass_y, pass_d, end, drain
-
-    res_start, res_x, res_y, res_d, res_end, res_drain = plane_gather(resg, re_m, 2)
+            rc(part, part, m.at[0], m.at[4], mate, c).wait_send()
+        return (start, functools.partial(relay, x_slot, 1), functools.partial(relay, y_slot, 2),
+                functools.partial(relay, d_slot, 3), end, drain)
+
+    res_start, res_x, res_y, res_d, res_end, res_drain = plane_gather(resg, re_m)
     res_start()
+    PL = PT * TILE
+    plane_lanes = pl.ds(pl.multiple_of(z * PL, PL), PL)
+    row_wait(p1g, p1_m)
     for q in range(nr):
-        gplane[:16, q * PT * TILE:(q + 1) * PT * TILE] = jnp.concatenate(
-            [gall[q, :, pl.ds(pl.multiple_of(z * PT * TILE, PT * TILE), PT * TILE)],
-             jnp.zeros((8, PT * TILE), f32)], axis=0).astype(bf16)
+        describe(gpl, slice(q * PL, (q + 1) * PL), line_of(p0g, q, 0, plane_lanes), line_of(p0g, q, 1, plane_lanes), support_mid)
+        lanes = slice(q * R1, (q + 1) * R1)
+        describe(gmid, lanes, line_of(p1g, q, 0), line_of(p1g, q, 1), support_mid)
+    gplane[:16] = gpl[...].astype(bf16)
+    gmids[:16] = gmid[...].astype(bf16)
 
     @pl.when(tmask_self)
     def _():
@@ -445,20 +440,19 @@
         wait_slots(tmask, nr, tm_m)
 
     block = pl.ds(pl.multiple_of(own_b * C1, C1), C1)
-    fbuf[0:8, :C1] = flipped_side(gmid[:, block])
+    fbuf[0:16, :C1] = flipped_side(gmid[:, block])
+    fbuf[0:16, C1:] = fbuf[0:16, :C1]
     for q in range(nr):
         for j in range(B1):
             fbuf[16 + q * PT:16 + (q + 1) * PT, j * TILE:(j + 1) * TILE] = tmask[q, j * PT:(j + 1) * PT, :]
-    own_tile = pl.ds(pl.multiple_of(own_b * C1 + (z * Q1) // TILE * TILE, TILE), TILE)
-    fbuf[0:8, C1:C1 + TILE] = flipped_side(gmid[:, own_tile])
-    for q in range(nr):
-        fbuf[16 + q * T1:16 + (q + 1) * T1, C1:C1 + TILE] = tmask[q, B1 * PT:B1 * PT + T1, :]
+            at = B1 * PT + j * T1
+            fbuf[16 + q * T1:16 + (q + 1) * T1, C1 + j * TILE:C1 + (j + 1) * TILE] = tmask[q, at:at + T1, :]
     side_t[...] = fbuf[...].T.astype(bf16)
 
     def put_e1t(lanes, value):
         e1t[:, lanes] = value
 
-    build(put_e1t, side_t.at[pl.ds(0, C1)], gplane, 16 + T0, support_mid, R0, 512)
+    build(put_e1t, side_t.at[pl.ds(0, C1)], gplane, 16 + T0, R0, 2048)
     row_wait(pcg, pc_m)
     row_wait(facg, f_m)
     res_x()
@@ -474,33 +468,34 @@
     col_send(lambda q: gtg.at[c], gtg.at[c], g_m)
     for t in range(NT2):
         line = pcg[per * t] + pcg[per * t + 1]
-        describe(gcoarse, slice(t * TILE, (t + 1) * TILE), line[0:1], line[1:2])
-    gcs[...] = jnp.concatenate([gcoarse[...], jnp.zeros((8, N2), f32)], axis=0).astype(bf16)
+        describe(gcoarse, slice(t * TILE, (t + 1) * TILE), line[0:1], line[1:2], support_coarse)
+    gcs[...] = gcoarse[...].astype(bf16)
+    for q in range(nr):
+        describe(gmid2, slice(q * R1, (q + 1) * R1), line_of(p1g, q, 0), line_of(p1g, q, 1), support_coarse)
     wide = fbuf.shape[1]
     for q in range(N1 // wide):
-        fbuf[0:8] = flipped_side(gmid[:, q * wide:(q + 1) * wide])
+        fbuf[0:16] = flipped_side(gmid2[:, q * wide:(q + 1) * wide])
         side_m[...] = fbuf[...].T.astype(bf16)
-        e2t[q * wide:(q + 1) * wide] = phi_of(dot(side_m[:, :16], gcs[...]), support_coarse)
+        e2t[q * wide:(q + 1) * wide] = phi_of(dot(side_m[:, :16], gcs[...]))
     res_d()
 
-    def put_a1t(lanes, value):
-        a1t[:, lanes] = value
-
-    own_half = pl.ds(pl.multiple_of(C1 + lax.rem(z * Q1, TILE), Q1), Q1)
-    build(put_a1t, side_t.at[own_half], gmids, 16 + NT1, support_mid, N1, 1024)
-    own_mids = pl.ds(pl.multiple_of(own_b * C1 + z * Q1, Q1), Q1)
-    coarse_gain = g["scale_e2"] * gain(support_coarse)
-    turned_w = coarse_gain * (e2t[own_mids, :].astype(f32)
-                              - (0.5 * g["scale_a1"] * gain(support_mid)) * dot(a1t[...], e2t[...]))
-    w_high, w_low = halves(turned_w)
-    w_pair = jnp.concatenate([w_high.astype(f32), w_low.astype(f32)], axis=0).T.astype(bf16)
-    wcat[:, :TILE] = w_pair
-    wcat[:, TILE:] = w_pair
+    restricted = jnp.zeros((C1, resg.shape[-1]), f32)
+    square = jnp.zeros((16, resg.shape[-1]), f32)
+
+    def restrict(slot):
+        strip_data = resg[slot]
+        held = strip_data.astype(f32)
+        return (dot(e1t[:, pl.ds(pl.multiple_of(slot * S0, S0), S0)], strip_data),
+                jnp.sum((held * held).reshape(S0 // 16, 16, -1), axis=0))
+
+    for slot in (own_b, x_slot, y_slot, d_slot):
+        term = restrict(slot)
+        restricted, square = restricted + term[0], square + term[1]
     res_end()
-    plane = resg[...].reshape(R0, -1)
-    restricted = dot(e1t[...], plane)
-    held = plane.astype(f32)
-    square = jnp.sum((held * held).reshape(R0 // 16, 16, -1), axis=0)
+    for slot in (2 * mate + h, 2 * mate + 1 - h, 2 * diag + h, 2 * yp + 1 - h):
+        term = restrict(slot)
+        restricted, square = restricted + term[0], square + term[1]
+    restricted = g["scale_e1"] * restricted
     for q in range(planes):
         part_buf[q] = jnp.concatenate([restricted[q * Q1:(q + 1) * Q1], square], axis=0).astype(bf16)
 
@@ -511,40 +506,14 @@
 
     z_send(lambda q: part_buf.at[q], rsin.at[z], rs_m)
     rsin[z] = part_buf[z]
-    wait_slots(emask, nc - 1, em_m)
-    fbuf[0:8, :S0] = flipped_side(gall[r, :, strip])
-    for q in range(nc):
-        for i in range(I0):
-            fbuf[16 + q * B1:16 + (q + 1) * B1, i * TILE:(i + 1) * TILE] = emask[q, i * B1:(i + 1) * B1, :]
-    side_e[...] = fbuf[:, :S0].T.astype(bf16)
-
-    def put_e1own(lanes, value):
-        e1own[:, lanes] = value
-
-    build(put_e1own, side_e, gmids, 16 + NT1, support_mid, N1, 512)
-    wait_slots(gtg, nc - 1, g_m)
-    gt = gtg[...].reshape(N2, N2)
-    gg_high, gg_low = halves(dot(gt.astype(f32).T.astype(bf16), gt))
-    zcat[S0 + C1:, :N2] = gg_high
-    zcat[S0 + C1:, N2:] = gg_low
-    fine_gain = g["scale_e1"] * gain(support_mid)
-    h_high, h_low = halves((fine_gain * coarse_gain) * dot(e1own[...], e2t[...]))
-    steps = (dot(h_high, gg_high) + dot(h_low, gg_high) + dot(h_high, gg_low),)
-    rows_c = e2t[pl.ds(pl.multiple_of(c * C1, C1), C1), :]
-    steps += (coarse_gain * (dot(rows_c, gg_high) + dot(rows_c, gg_low)),)
-    for k, step in enumerate(steps):
-        high, low = halves(step)
-        zcat[k * C1:(k + 1) * C1, :N2] = high
-        zcat[k * C1:(k + 1) * C1, N2:] = low
-
-    wait_slots(rsin, planes - 1, rs_m)
-    total = rsin[0].astype(f32)
-    for q in range(1, planes):
-        total = total + rsin[q].astype(f32)
-    q_high, q_low = halves(fine_gain * total[:Q1])
-    part = dot(wcat[...], jnp.concatenate([q_high, q_high, q_low, q_low], axis=0))
-    csend[...] = part.reshape(D, CR, -1).astype(bf16)
-
+    def put_a1t(lanes, value):
+        a1t[:, lanes] = value
+
+    build(put_a1t, side_t.at[pl.ds(C1, C1)], gmids, 16 + NT1, N1, 1024)
+    turned_w = g["scale_e2"] * (e2t[block, :].astype(f32) - (0.5 * g["scale_a1"]) * dot(a1t[...], e2t[...]))
+    w_high, w_low = halves(turned_w.T)
+    for k, w in enumerate((w_high, w_low, w_high)):
+        wcat[:, k * C1:(k + 1) * C1] = w
     def all_send(src_of, dst, m):
         def go(k):
             q = lax.rem(c + k, nc)
@@ -556,29 +525,64 @@
             p = lax.rem(r + j, nr)
             rc(src_of(p * nc + c), dst, m.at[0], m.at[1], p, c).start()
 
+    part_high, part_low = halves(restricted)
+    part = dot(wcat[...], jnp.concatenate([part_high, part_high, part_low], axis=0))
+    csend[...] = part.reshape(D, CR, -1).astype(bf16)
     all_send(lambda q: csend.at[q], crecv.at[d], cr_m)
+    crecv[d] = csend[d]
+    wait_slots(emask, nc - 1, em_m)
+    describe(gstrip, slice(None), line_of(p0g, r, 0, strip), line_of(p0g, r, 1, strip), support_mid)
+    fbuf[0:16, :S0] = flipped_side(gstrip[...])
+    for q in range(nc):
+        for i in range(I0):
+            fbuf[16 + q * B1:16 + (q + 1) * B1, i * TILE:(i + 1) * TILE] = emask[q, i * B1:(i + 1) * B1, :]
+    side_e[...] = fbuf[:, :S0].T.astype(bf16)
+
+    def put_e1own(lanes, value):
+        e1own[:, lanes] = value
+
+    build(put_e1own, side_e, gmids, 16 + NT1, N1, 2048)
+    fine_gain = g["scale_e1"]
+    wait_slots(rsin, planes - 1, rs_m)
+    total = rsin[0].astype(f32)
+    for q in range(1, planes):
+        total = total + rsin[q].astype(f32)
+    q_high = total[:Q1].astype(bf16)
     mida[own_b, z] = q_high
     z_send(lambda q: mida.at[own_b, z], mida.at[own_b, z], mz_m)
-    crecv[d] = csend[d]
-    norm_o[...] = jnp.broadcast_to(jnp.sum(total[Q1:], keepdims=True) * g["norm_scale"], norm_o.shape)
+    wait_slots(gtg, nc - 1, g_m)
+    gt = gtg[...].reshape(N2, N2)
+    gg_high, gg_low = halves(dot(gt.astype(f32).T.astype(bf16), gt))
+    zcat[S0 + C1:, :N2] = gg_high
+    zcat[S0 + C1:, N2:] = gg_low
+    h_high, h_low = halves((fine_gain * g["scale_e2"]) * dot(e1own[...], e2t[...]))
+    steps = (dot(h_high, gg_high) + dot(h_low, gg_high) + dot(h_high, gg_low),)
+    rows_c = e2t[pl.ds(pl.multiple_of(c * C1, C1), C1), :]
+    steps += (g["scale_e2"] * (dot(rows_c, gg_high) + dot(rows_c, gg_low)),)
+    for k, step in enumerate(steps):
+        high, low = halves(step)
+        zcat[k * C1:(k + 1) * C1, :N2] = high
+        zcat[k * C1:(k + 1) * C1, N2:] = low
+
     wait_slots(crecv, D - 1, cr_m)
     cg[d] = jnp.sum(crecv[...].astype(f32), axis=0).astype(bf16)
     all_send(lambda q: cg.at[d], cg.at[d], ca_m)
-    mid_start, mid_x, mid_y, mid_d, mid_end, mid_drain = plane_gather(mida, ma_m, planes)
+    mid_start, mid_x, mid_y, mid_d, mid_end, mid_drain = plane_gather(mida, ma_m)
+    norm_o[...] = jnp.broadcast_to(jnp.sum(total[Q1:], keepdims=True) * g["norm_scale"], norm_o.shape)
     arrived = mida.at[own_b, pl.ds(0, planes - 1)]
     rc(arrived, arrived, mz_m.at[0], mz_m.at[1], mate, c).wait()
     mid_start()
     mid_x()
     mid_y()
+    mid_d()
     wait_slots(cg, D - 1, ca_m)
     cd = cg[...].astype(f32).reshape(N2, -1).astype(bf16)
     both = jnp.concatenate([cd, cd], axis=0)
     coarse_o[...] = dot(zcat[pl.ds(pl.multiple_of(S0 + C1 + r * R2, R2), R2), :], both)
-    mid_d()
+    step = dot(zcat[:S0 + C1, :], both)
     mid_end()
-    mid_o[...] = 0.5 * mida[c].astype(f32).reshape(C1, -1) + dot(zcat[S0:S0 + C1, :], both)
-    fine_o[...] = (0.5 * own_vals + (0.5 * fine_gain) * dot(e1own[...], mida[...].reshape(N1, -1))
-                   + dot(zcat[:S0, :], both))
+    mid_o[...] = 0.5 * mida[c].astype(f32).reshape(C1, -1) + step[S0:]
+    fine_o[...] = 0.5 * own_vals + (0.5 * fine_gain) * dot(e1own[...], mida[...].reshape(N1, -1)) + step[:S0]
     res_drain()
     mid_drain()
 
@@ -628,17 +632,17 @@
         V((nc, I0 * B0, TILE), bf16), V((nc, 8, TILE), f32), V((nr, 16, TILE), f32),
         V((nc, I0 * B0, TILE), bf16), V((nc, 8, TILE), f32), V((planes, 16, TILE), f32),
         V((wide, TILE), bf16), V((nr, wide, TILE), bf16), V((nc, wide, N2), bf16),
-        V((nr, 8, R0), f32), V((8, N1), f32), V((8, N2), f32),
+        V((2, 16, R0), f32), V((16, S0), f32), V((16, R0), f32), V((16, N1), f32), V((16, N1), f32), V((16, N2), f32),
         V((16 + 2 * T0, 2 * R0), bf16), V((16 + T0, R0), bf16), V((16 + nr * T1, N1), bf16), V((16, N2), bf16),
         V((TILE, 2 * S0), f32), V((2 * S0, TILE), bf16), V((S0, TILE), bf16), V((2 * S0, TILE), bf16),
         V((8, TILE), bf16), V((2 * S0, TILE), bf16),
-        V((2, S0, 2 * R0), bf16), V((S0, N1), bf16), V((C1, R0), bf16), V((N1, N2), bf16), V((Q1, N1), bf16),
-        V((S0, F), bf16), V((S0, F), bf16), V((nc, 2, S0 // 2, F), bf16),
+        V((2, S0, 2 * R0), bf16), V((S0, N1), bf16), V((C1, R0), bf16), V((N1, N2), bf16), V((C1, N1), bf16),
+        V((S0, F), bf16), V((S0, F), bf16), V((nc, S0, F), bf16),
         V((planes, Q1 + 16, F), bf16), V((planes, Q1 + 16, F), bf16), V((nc, planes, Q1, F), bf16),
-        V((D, CR, F), bf16), V((D, CR, F), bf16), V((D, CR, F), bf16), V((N2, 4 * Q1), bf16),
+        V((D, CR, F), bf16), V((D, CR, F), bf16), V((D, CR, F), bf16), V((N2, 3 * C1), bf16),
         V((S0 + C1 + N2, 2 * N2), bf16),
     ]
-    for n in (8, 2, 2, 2, 2, 2, 2, 2, 2, 2, 2, 6, 2, 2, 6, 2, 2):
+    for n in (8, 2, 2, 2, 2, 2, 2, 2, 2, 2, 2, 5, 2, 2, 5, 2, 2):
         scratch += [dma((n,))]
     vm = pl.BlockSpec(memory_space=pltpu.VMEM)
     shapes = ((S0, F), (C1, F), (R2, F))

time: 44.8 us -> 39 us (0.87)
  Pallas kernels: 43.6 us -> 38.1 us
    pallas_call x1, Pallas kernels: 42.8 us -> 37.4 us  [fused(): pl.pallas_call(functools.partial(cycle_kernel, g), out_shape=tuple((jax.S...]
where the time goes in v4:
time: 39 us; the launch traced here: 38.8 us
  Pallas kernels  38.1 us (98%)
  between operations  0.64 us (2%)
    pallas_call x1, Pallas kernels, fused(): pl.pallas_call(functools.partial(cycle_kernel, g), out_shape=tuple((jax.S...  37.4 us

profile of v4, /device:TPU:0, one launch (start us, length us, event | category | flops | bytes accessed | tf_op | source)
XLA Modules:
  0.0 38.8 jit_solution(4943690538116714669)
XLA Ops:
  0.6 37.4 %shard_map.111 = (f32[256,128]{1,0:T(8,128)S(1)}, f32[256,128]{1,0:T(8,128)S(1)}, f32[64,128]{1,0:T(8,128)S(1)}, f32[8,128]{1,0:T(8,128)S(1)}) custom-call(bf16[2048,128]{1,0:T(8,128)(2,1)} %vals_h.1, bf16[2,2048]{1,0:T(2,128)(2,1)} %points0_h.1, bf16[2,512]{1,0:T(2,128)(2,1)} %points1_h.1, bf16[2,64]{1,0:T(2,128)(2,1)} %points2_h.1, ...), custom_call_target="tpu_custom_call" | custom-call | tf_op jit(solution)/shard_map/pallas_call | solution.py:649
  38.0 0.7 %shard_map.112 = (f32[256,128]{1,0:T(8,128)}, f32[256,128]{1,0:T(8,128)}, f32[64,128]{1,0:T(8,128)}, f32[1,1]{1,0:T(1,128)}) custom-call(f32[256,128]{1,0:T(8,128)S(1)} %get-tuple-element.12.fine, f32[256,128]{1,0:T(8,128)S(1)} %get-tuple-element.13.mid, f32[64,128]{1,0:T(8,128)S(1)} %get-tuple-element.14.coarse, f32[8,128]{1,0:T(8,128)S(1)} %get-tuple-element.15.norm), custom_call_target="tpu_custom_call" | custom-call | tf_op jit(solution)/shard_map/pallas_call | solution.py:658

commit v5 on v4

--- a/solution.py
+++ b/solution.py
@@ -382,45 +382,73 @@
         return put
 
     KA = 16 + 2 * T0
-    build(put_a0(1), side_a.at[pl.ds(S0, S0)], gfine, KA, 2 * R0, 2048)
-    rc(v2.at[1 - k_core], v2.at[1 - k_core], v_m.at[0], v_m.at[1], mate, c).wait()
-    other_s[...] = (dot(a0[1, :, :R0], v2[0]) + dot(a0[1, :, R0:], v2[1])).astype(bf16)
-    rc(other_s, other_r, ot_m.at[0], ot_m.at[1], yp, c).start()
-    build(put_a0(0), side_a.at[pl.ds(0, S0)], gfine, KA, 2 * R0, 2048)
-    acc = dot(a0[0, :, :R0], v2[0]) + dot(a0[0, :, R0:], v2[1])
+    def product(s, lo, hi):
+        total = None
+        for k in range(2):
+            lanes = slice(k * R0, (k + 1) * R0)
+            a0[s, lo:hi, lanes] = phi_of(dot(side_a[s * S0 + lo:s * S0 + hi, :KA], gfine[:KA, lanes]))
+            if s == 1 and lo == 0 and k == 0:
+                rc(v2.at[1 - k_core], v2.at[1 - k_core], v_m.at[0], v_m.at[1], mate, c).wait()
+            term = dot(a0[s, lo:hi, lanes], v2[k])
+            total = term if total is None else total + term
+        return total
+
+    def other_copy(i):
+        rows = pl.ds(i * TILE, TILE)
+        return rc(other_s.at[rows], other_r.at[rows], ot_m.at[0], ot_m.at[1 + i], yp, c)
+
+    for i in range(I0):
+        other_s[i * TILE:(i + 1) * TILE] = product(1, i * TILE, (i + 1) * TILE).astype(bf16)
+        other_copy(i).start()
+    acc = product(0, 0, S0)
     own_vals = v2[k_core, strip, :].astype(f32)
-    rc(other_s, other_r, ot_m.at[0], ot_m.at[1], yp, c).wait()
-    res = own_vals - (0.5 * g["scale_a0"]) * (acc + other_r[...].astype(f32))
-    resg[own_b] = res.astype(bf16)
-
     x_slot, y_slot, d_slot = 2 * r + 1 - h, 2 * yp + h, 2 * diag + 1 - h
 
-    def plane_gather(ref, m):
+    def plane_gather(at, m, base, mate_sem):
         def send(slot, sem, rr, cc):
-            rc(ref.at[slot], ref.at[slot], m.at[0], m.at[sem], rr, cc).start()
+            rc(at(slot), at(slot), m.at[0], m.at[sem], rr, cc).start()
 
         def start():
-            send(own_b, 1, r, xp)
-            send(own_b, 2, yp, c)
-            send(own_b, 3, diag, xp)
-            send(own_b, 4, mate, c)
+            send(own_b, base, r, xp)
+            send(own_b, base + 1, yp, c)
+            send(own_b, base + 2, diag, xp)
+            send(own_b, mate_sem, mate, c)
 
         def relay(slot, sem):
-            rc(ref.at[slot], ref.at[slot], m.at[0], m.at[sem], mate, c).wait_recv()
-            send(slot, 4, mate, c)
-
-        def end():
-            part = ref.at[pl.ds(0, 4)]
-            rc(part, part, m.at[0], m.at[4], mate, c).wait_recv()
-
-        def drain():
-            part = ref.at[pl.ds(0, 7)]
-            rc(part, part, m.at[0], m.at[4], mate, c).wait_send()
-        return (start, functools.partial(relay, x_slot, 1), functools.partial(relay, y_slot, 2),
-                functools.partial(relay, d_slot, 3), end, drain)
-
-    res_start, res_x, res_y, res_d, res_end, res_drain = plane_gather(resg, re_m)
-    res_start()
+            rc(at(slot), at(slot), m.at[0], m.at[sem], mate, c).wait_recv()
+            send(slot, mate_sem, mate, c)
+
+        return (start, functools.partial(relay, x_slot, base), functools.partial(relay, y_slot, base + 1),
+                functools.partial(relay, d_slot, base + 2))
+
+    def plane_end(ref, m, mate_sem):
+        part = ref.at[pl.ds(0, 4)]
+        rc(part, part, m.at[0], m.at[mate_sem], mate, c).wait_recv()
+
+    def plane_drain(ref, m, mate_sem):
+        part = ref.at[pl.ds(0, 7)]
+        rc(part, part, m.at[0], m.at[mate_sem], mate, c).wait_send()
+
+    def all_send(src_of, dst, m):
+        def go(k):
+            q = lax.rem(c + k, nc)
+            for j in range(nr):
+                p = lax.rem(r + j, nr)
+                rc(src_of(p * nc + q), dst, m.at[0], m.at[1], p, q).start()
+        each(1, nc, go)
+        for j in range(1, nr):
+            p = lax.rem(r + j, nr)
+            rc(src_of(p * nc + c), dst, m.at[0], m.at[1], p, c).start()
+
+    def res_part(i):
+        return plane_gather(lambda slot: resg.at[slot, pl.ds(i * TILE, TILE)], re_m, 1 + 3 * i, 7)
+
+    res_parts = [res_part(i) for i in range(I0)]
+    for i in range(I0):
+        other_copy(i).wait_recv()
+        rows = slice(i * TILE, (i + 1) * TILE)
+        resg[own_b, rows] = (own_vals[rows] - (0.5 * g["scale_a0"]) * (acc[rows] + other_r[rows].astype(f32))).astype(bf16)
+        res_parts[i][0]()
     PL = PT * TILE
     plane_lanes = pl.ds(pl.multiple_of(z * PL, PL), PL)
     row_wait(p1g, p1_m)
@@ -455,8 +483,12 @@
     build(put_e1t, side_t.at[pl.ds(0, C1)], gplane, 16 + T0, R0, 2048)
     row_wait(pcg, pc_m)
     row_wait(facg, f_m)
-    res_x()
-    res_y()
+    def put_a1t(lanes, value):
+        a1t[:, lanes] = value
+
+    build(put_a1t, side_t.at[pl.ds(C1, C1)], gmids, 16 + NT1, N1, 1024)
+    for k in range(1, 4):
+        res_parts[0][k]()
     strips = []
     per = TILE // R2
     for lane in range(NT2):
@@ -477,8 +509,8 @@
         fbuf[0:16] = flipped_side(gmid2[:, q * wide:(q + 1) * wide])
         side_m[...] = fbuf[...].T.astype(bf16)
         e2t[q * wide:(q + 1) * wide] = phi_of(dot(side_m[:, :16], gcs[...]))
-    res_d()
-
+    for k in range(1, 4):
+        res_parts[1][k]()
     restricted = jnp.zeros((C1, resg.shape[-1]), f32)
     square = jnp.zeros((16, resg.shape[-1]), f32)
 
@@ -491,7 +523,7 @@
     for slot in (own_b, x_slot, y_slot, d_slot):
         term = restrict(slot)
         restricted, square = restricted + term[0], square + term[1]
-    res_end()
+    plane_end(resg, re_m, 7)
     for slot in (2 * mate + h, 2 * mate + 1 - h, 2 * diag + h, 2 * yp + 1 - h):
         term = restrict(slot)
         restricted, square = restricted + term[0], square + term[1]
@@ -506,24 +538,10 @@
 
     z_send(lambda q: part_buf.at[q], rsin.at[z], rs_m)
     rsin[z] = part_buf[z]
-    def put_a1t(lanes, value):
-        a1t[:, lanes] = value
-
-    build(put_a1t, side_t.at[pl.ds(C1, C1)], gmids, 16 + NT1, N1, 1024)
     turned_w = g["scale_e2"] * (e2t[block, :].astype(f32) - (0.5 * g["scale_a1"]) * dot(a1t[...], e2t[...]))
     w_high, w_low = halves(turned_w.T)
     for k, w in enumerate((w_high, w_low, w_high)):
         wcat[:, k * C1:(k + 1) * C1] = w
-    def all_send(src_of, dst, m):
-        def go(k):
-            q = lax.rem(c + k, nc)
-            for j in range(nr):
-                p = lax.rem(r + j, nr)
-                rc(src_of(p * nc + q), dst, m.at[0], m.at[1], p, q).start()
-        each(1, nc, go)
-        for j in range(1, nr):
-            p = lax.rem(r + j, nr)
-            rc(src_of(p * nc + c), dst, m.at[0], m.at[1], p, c).start()
 
     part_high, part_low = halves(restricted)
     part = dot(wcat[...], jnp.concatenate([part_high, part_high, part_low], axis=0))
@@ -549,7 +567,20 @@
         total = total + rsin[q].astype(f32)
     q_high = total[:Q1].astype(bf16)
     mida[own_b, z] = q_high
-    z_send(lambda q: mida.at[own_b, z], mida.at[own_b, z], mz_m)
+    own_q = mida.at[own_b, z]
+    near_z = z + 1 - 2 * lax.rem(z, 2)
+    rc(own_q, own_q, mz_m.at[0], mz_m.at[1], r, 2 * near_z + h).start()
+    rank = jnp.where((z == 0) | (z == planes - 1), 3, 2)
+    for k in range(2):
+        q = jnp.where(z < 2, 2 + k, k)
+        rc(own_q, own_q, mz_m.at[0], mz_m.at[rank], r, 2 * q + h).start()
+    order = (z, near_z, jnp.where(z < 2, 2, 1), jnp.where(z < 2, 3, 0))
+
+    def batch(k):
+        return plane_gather(lambda slot: mida.at[slot, order[k]], ma_m, 1 + 3 * k, 13)
+
+    batches = [batch(k) for k in range(planes)]
+    batches[0][0]()
     wait_slots(gtg, nc - 1, g_m)
     gt = gtg[...].reshape(N2, N2)
     gg_high, gg_low = halves(dot(gt.astype(f32).T.astype(bf16), gt))
@@ -564,27 +595,36 @@
         zcat[k * C1:(k + 1) * C1, :N2] = high
         zcat[k * C1:(k + 1) * C1, N2:] = low
 
+    def z_take(k):
+        piece = mida.at[own_b, order[k]]
+        rc(piece, piece, mz_m.at[0], mz_m.at[k], mate, c).wait_recv()
+        batches[k][0]()
+
     wait_slots(crecv, D - 1, cr_m)
     cg[d] = jnp.sum(crecv[...].astype(f32), axis=0).astype(bf16)
     all_send(lambda q: cg.at[d], cg.at[d], ca_m)
-    mid_start, mid_x, mid_y, mid_d, mid_end, mid_drain = plane_gather(mida, ma_m)
+    for k in range(1, 4):
+        batches[0][k]()
+    z_take(1)
+    z_take(2)
+    z_take(3)
     norm_o[...] = jnp.broadcast_to(jnp.sum(total[Q1:], keepdims=True) * g["norm_scale"], norm_o.shape)
-    arrived = mida.at[own_b, pl.ds(0, planes - 1)]
-    rc(arrived, arrived, mz_m.at[0], mz_m.at[1], mate, c).wait()
-    mid_start()
-    mid_x()
-    mid_y()
-    mid_d()
+    for b in batches[1:]:
+        for k in range(1, 4):
+            b[k]()
     wait_slots(cg, D - 1, ca_m)
     cd = cg[...].astype(f32).reshape(N2, -1).astype(bf16)
     both = jnp.concatenate([cd, cd], axis=0)
     coarse_o[...] = dot(zcat[pl.ds(pl.multiple_of(S0 + C1 + r * R2, R2), R2), :], both)
     step = dot(zcat[:S0 + C1, :], both)
-    mid_end()
+    plane_end(mida, ma_m, 13)
     mid_o[...] = 0.5 * mida[c].astype(f32).reshape(C1, -1) + step[S0:]
     fine_o[...] = 0.5 * own_vals + (0.5 * fine_gain) * dot(e1own[...], mida[...].reshape(N1, -1)) + step[:S0]
-    res_drain()
-    mid_drain()
+    rc(other_s, other_r, ot_m.at[0], ot_m.at[1], yp, c).wait_send()
+    plane_drain(resg, re_m, 7)
+    plane_drain(mida, ma_m, 13)
+    held_z = mida.at[own_b, pl.ds(0, planes - 1)]
+    rc(held_z, held_z, mz_m.at[0], mz_m.at[1], mate, c).wait_send()
 
 
 def finish_kernel(fine, mid, coarse, norm, fine_o, mid_o, coarse_o, norm_o):
@@ -642,7 +682,7 @@
         V((D, CR, F), bf16), V((D, CR, F), bf16), V((D, CR, F), bf16), V((N2, 3 * C1), bf16),
         V((S0 + C1 + N2, 2 * N2), bf16),
     ]
-    for n in (8, 2, 2, 2, 2, 2, 2, 2, 2, 2, 2, 5, 2, 2, 5, 2, 2):
+    for n in (8, 2, 2, 2, 2, 2, 2, 2, 2, 2, 1 + I0, 2 + 3 * I0, 2, 4, 14, 2, 2):
         scratch += [dma((n,))]
     vm = pl.BlockSpec(memory_space=pltpu.VMEM)
     shapes = ((S0, F), (C1, F), (R2, F))

time: 39 us -> 36.8 us (0.944)
  Pallas kernels: 38.1 us -> 36 us
    pallas_call x1, Pallas kernels: 37.4 us -> 35.3 us  [fused(): pl.pallas_call(functools.partial(cycle_kernel, g), out_shape=tuple((jax.S...]
where the time goes in v5:
time: 36.8 us; the launch traced here: 36.6 us
  Pallas kernels  36 us (98%)
  between operations  0.64 us (2%)
    pallas_call x1, Pallas kernels, fused(): pl.pallas_call(functools.partial(cycle_kernel, g), out_shape=tuple((jax.S...  35.3 us

profile of v5, /device:TPU:0, one launch (start us, length us, event | category | flops | bytes accessed | tf_op | source)
XLA Modules:
  0.0 36.6 jit_solution(11484920207716191119)
XLA Ops:
  0.6 35.3 %shard_map.111 = (f32[256,128]{1,0:T(8,128)S(1)}, f32[256,128]{1,0:T(8,128)S(1)}, f32[64,128]{1,0:T(8,128)S(1)}, f32[8,128]{1,0:T(8,128)S(1)}) custom-call(bf16[2048,128]{1,0:T(8,128)(2,1)} %vals_h.1, bf16[2,2048]{1,0:T(2,128)(2,1)} %points0_h.1, bf16[2,512]{1,0:T(2,128)(2,1)} %points1_h.1, bf16[2,64]{1,0:T(2,128)(2,1)} %points2_h.1, ...), custom_call_target="tpu_custom_call" | custom-call | tf_op jit(solution)/shard_map/pallas_call | solution.py:689
  35.9 0.7 %shard_map.112 = (f32[256,128]{1,0:T(8,128)}, f32[256,128]{1,0:T(8,128)}, f32[64,128]{1,0:T(8,128)}, f32[1,1]{1,0:T(1,128)}) custom-call(f32[256,128]{1,0:T(8,128)S(1)} %get-tuple-element.12.fine, f32[256,128]{1,0:T(8,128)S(1)} %get-tuple-element.13.mid, f32[64,128]{1,0:T(8,128)S(1)} %get-tuple-element.14.coarse, f32[8,128]{1,0:T(8,128)S(1)} %get-tuple-element.15.norm), custom_call_target="tpu_custom_call" | custom-call | tf_op jit(solution)/shard_map/pallas_call | solution.py:698

commit v6 on v5

--- a/solution.py
+++ b/solution.py
@@ -190,8 +190,8 @@
                  tiles_a0, tiles_e1, tiles_a1, factor, points2,
                  v2, p0g, p1g, pcg, maskg, emask, tmask, masks_s, emask_s, tmask_s, fac, facg, gtg,
                  gall, gstrip, gpl, gmid, gmid2, gcoarse, gfine, gplane, gmids, gcs, fbuf, side_a, side_e, side_t, side_o, side_m,
-                 a0, e1own, e1t, e2t, a1t, other_s, other_r, resg, part_buf, rsin, mida, csend, crecv, cg, wcat, zcat,
-                 l_s, a_m, p0_m, p1_m, pc_m, v_m, em_m, tm_m, f_m, g_m, ot_m, re_m, rs_m, mz_m, ma_m, cr_m, ca_m):
+                 a0, e1own, e1t, e2t, a1t, other_s, other_r, resg, part_buf, rsin, square_g, mida, csend, crecv, cg, wcat, zcat,
+                 l_s, a_m, p0_m, p1_m, pc_m, v_m, em_m, tm_m, f_m, g_m, ot_m, re_m, rs_m, sq_m, mz_m, ma_m, cr_m, ca_m):
     nr, nc, R0, R1, R2 = g["nr"], g["nc"], g["R0"], g["R1"], g["R2"]
     D = nr * nc
     T0, T1 = R0 // TILE, R1 // TILE
@@ -409,9 +409,9 @@
             rc(at(slot), at(slot), m.at[0], m.at[sem], rr, cc).start()
 
         def start():
+            send(own_b, base + 2, diag, xp)
+            send(own_b, base + 1, yp, c)
             send(own_b, base, r, xp)
-            send(own_b, base + 1, yp, c)
-            send(own_b, base + 2, diag, xp)
             send(own_b, mate_sem, mate, c)
 
         def relay(slot, sem):
@@ -529,15 +529,18 @@
         restricted, square = restricted + term[0], square + term[1]
     restricted = g["scale_e1"] * restricted
     for q in range(planes):
-        part_buf[q] = jnp.concatenate([restricted[q * Q1:(q + 1) * Q1], square], axis=0).astype(bf16)
+        part_buf[q] = restricted[q * Q1:(q + 1) * Q1].astype(bf16)
+
+    near_z = z + 1 - 2 * lax.rem(z, 2)
+    far_first = (jnp.where(z < 2, 3, 0), jnp.where(z < 2, 2, 1), near_z)
 
     def z_send(src_of, dst, m):
-        for k in range(1, planes):
-            q = lax.rem(z + k, planes)
+        for q in far_first:
             rc(src_of(q), dst, m.at[0], m.at[1], r, 2 * q + h).start()
 
     z_send(lambda q: part_buf.at[q], rsin.at[z], rs_m)
     rsin[z] = part_buf[z]
+    square_g[z] = square.astype(bf16)
     turned_w = g["scale_e2"] * (e2t[block, :].astype(f32) - (0.5 * g["scale_a1"]) * dot(a1t[...], e2t[...]))
     w_high, w_low = halves(turned_w.T)
     for k, w in enumerate((w_high, w_low, w_high)):
@@ -565,22 +568,20 @@
     total = rsin[0].astype(f32)
     for q in range(1, planes):
         total = total + rsin[q].astype(f32)
-    q_high = total[:Q1].astype(bf16)
+    q_high = total.astype(bf16)
     mida[own_b, z] = q_high
     own_q = mida.at[own_b, z]
-    near_z = z + 1 - 2 * lax.rem(z, 2)
-    rc(own_q, own_q, mz_m.at[0], mz_m.at[1], r, 2 * near_z + h).start()
     rank = jnp.where((z == 0) | (z == planes - 1), 3, 2)
-    for k in range(2):
-        q = jnp.where(z < 2, 2 + k, k)
-        rc(own_q, own_q, mz_m.at[0], mz_m.at[rank], r, 2 * q + h).start()
-    order = (z, near_z, jnp.where(z < 2, 2, 1), jnp.where(z < 2, 3, 0))
+    for q, sem in ((far_first[0], rank), (far_first[1], rank), (near_z, 1)):
+        rc(own_q, own_q, mz_m.at[0], mz_m.at[sem], r, 2 * q + h).start()
+    order = (z,) + far_first[::-1]
 
     def batch(k):
         return plane_gather(lambda slot: mida.at[slot, order[k]], ma_m, 1 + 3 * k, 13)
 
     batches = [batch(k) for k in range(planes)]
     batches[0][0]()
+    z_send(lambda q: square_g.at[z], square_g.at[z], sq_m)
     wait_slots(gtg, nc - 1, g_m)
     gt = gtg[...].reshape(N2, N2)
     gg_high, gg_low = halves(dot(gt.astype(f32).T.astype(bf16), gt))
@@ -608,7 +609,8 @@
     z_take(1)
     z_take(2)
     z_take(3)
-    norm_o[...] = jnp.broadcast_to(jnp.sum(total[Q1:], keepdims=True) * g["norm_scale"], norm_o.shape)
+    wait_slots(square_g, planes - 1, sq_m)
+    norm_o[...] = jnp.broadcast_to(jnp.sum(square_g[...].astype(f32), keepdims=True).reshape(1, 1) * g["norm_scale"], norm_o.shape)
     for b in batches[1:]:
         for k in range(1, 4):
             b[k]()
@@ -617,9 +619,15 @@
     both = jnp.concatenate([cd, cd], axis=0)
     coarse_o[...] = dot(zcat[pl.ds(pl.multiple_of(S0 + C1 + r * R2, R2), R2), :], both)
     step = dot(zcat[:S0 + C1, :], both)
+    def prolong(slot):
+        return dot(e1own[:, pl.ds(pl.multiple_of(slot * C1, C1), C1)], mida[slot].reshape(C1, -1))
+
+    base = prolong(own_b) + prolong(x_slot) + prolong(y_slot) + prolong(d_slot)
     plane_end(mida, ma_m, 13)
+    for slot in (2 * mate + h, 2 * mate + 1 - h, 2 * diag + h, 2 * yp + 1 - h):
+        base = base + prolong(slot)
     mid_o[...] = 0.5 * mida[c].astype(f32).reshape(C1, -1) + step[S0:]
-    fine_o[...] = 0.5 * own_vals + (0.5 * fine_gain) * dot(e1own[...], mida[...].reshape(N1, -1)) + step[:S0]
+    fine_o[...] = 0.5 * own_vals + (0.5 * fine_gain) * base + step[:S0]
     rc(other_s, other_r, ot_m.at[0], ot_m.at[1], yp, c).wait_send()
     plane_drain(resg, re_m, 7)
     plane_drain(mida, ma_m, 13)
@@ -678,11 +686,11 @@
         V((8, TILE), bf16), V((2 * S0, TILE), bf16),
         V((2, S0, 2 * R0), bf16), V((S0, N1), bf16), V((C1, R0), bf16), V((N1, N2), bf16), V((C1, N1), bf16),
         V((S0, F), bf16), V((S0, F), bf16), V((nc, S0, F), bf16),
-        V((planes, Q1 + 16, F), bf16), V((planes, Q1 + 16, F), bf16), V((nc, planes, Q1, F), bf16),
+        V((planes, Q1, F), bf16), V((planes, Q1, F), bf16), V((planes, 16, F), bf16), V((nc, planes, Q1, F), bf16),
         V((D, CR, F), bf16), V((D, CR, F), bf16), V((D, CR, F), bf16), V((N2, 3 * C1), bf16),
         V((S0 + C1 + N2, 2 * N2), bf16),
     ]
-    for n in (8, 2, 2, 2, 2, 2, 2, 2, 2, 2, 1 + I0, 2 + 3 * I0, 2, 4, 14, 2, 2):
+    for n in (8, 2, 2, 2, 2, 2, 2, 2, 2, 2, 1 + I0, 2 + 3 * I0, 2, 2, 4, 14, 2, 2):
         scratch += [dma((n,))]
     vm = pl.BlockSpec(memory_space=pltpu.VMEM)
     shapes = ((S0, F), (C1, F), (R2, F))

time: 36.8 us -> 36 us (0.978)
  Pallas kernels: 36 us -> 35.2 us
    pallas_call x1, Pallas kernels: 35.3 us -> 34.5 us  [fused(): pl.pallas_call(functools.partial(cycle_kernel, g), out_shape=tuple((jax.S...]
where the time goes in v6:
time: 36 us; the launch traced here: 35.8 us
  Pallas kernels  35.2 us (98%)
  between operations  0.64 us (2%)
    pallas_call x1, Pallas kernels, fused(): pl.pallas_call(functools.partial(cycle_kernel, g), out_shape=tuple((jax.S...  34.5 us
    pallas_call x1, Pallas kernels, fused(): pl.pallas_call(finish_kernel, grid=(1,), out_shape=tuple((jax.ShapeDtypeS...  0.72 us

profile of v6, /device:TPU:0, one launch (start us, length us, event | category | flops | bytes accessed | tf_op | source)
XLA Modules:
  0.0 35.8 jit_solution(11812071548269145255)
XLA Ops:
  0.6 34.5 %shard_map.111 = (f32[256,128]{1,0:T(8,128)S(1)}, f32[256,128]{1,0:T(8,128)S(1)}, f32[64,128]{1,0:T(8,128)S(1)}, f32[8,128]{1,0:T(8,128)S(1)}) custom-call(bf16[2048,128]{1,0:T(8,128)(2,1)} %vals_h.1, bf16[2,2048]{1,0:T(2,128)(2,1)} %points0_h.1, bf16[2,512]{1,0:T(2,128)(2,1)} %points1_h.1, bf16[2,64]{1,0:T(2,128)(2,1)} %points2_h.1, ...), custom_call_target="tpu_custom_call" | custom-call | tf_op jit(solution)/shard_map/pallas_call | solution.py:697
  35.1 0.7 %shard_map.112 = (f32[256,128]{1,0:T(8,128)}, f32[256,128]{1,0:T(8,128)}, f32[64,128]{1,0:T(8,128)}, f32[1,1]{1,0:T(1,128)}) custom-call(f32[256,128]{1,0:T(8,128)S(1)} %get-tuple-element.12.fine, f32[256,128]{1,0:T(8,128)S(1)} %get-tuple-element.13.mid, f32[64,128]{1,0:T(8,128)S(1)} %get-tuple-element.14.coarse, f32[8,128]{1,0:T(8,128)S(1)} %get-tuple-element.15.norm), custom_call_target="tpu_custom_call" | custom-call | tf_op jit(solution)/shard_map/pallas_call | solution.py:706

commit v7 on v6

--- a/solution.py
+++ b/solution.py
@@ -297,21 +297,25 @@
     mask_slot = jnp.where(y_of == y, 0, 1) * planes + lax.rem(c, planes)
     mask_self = y_of == y
 
-    def mask_go(k):
-        q = lax.rem(c + k, nc)
+    def mask_go_to(q):
         rc(masks_s.at[q], maskg.at[mask_slot], a_m.at[0], a_m.at[1], mask_row, q).start()
 
-    each(1, nc, mask_go)
+    near_z = z + 1 - 2 * lax.rem(z, 2)
+    far_first = (jnp.where(z < 2, 3, 0), jnp.where(z < 2, 2, 1), near_z)
+    row_send(p0g.at[r], p0g.at[r], p0_m)
+    for q in far_first:
+        for j in range(2):
+            mask_go_to(2 * q + j)
+    mask_go_to(xp)
 
     @pl.when(jnp.logical_not(mask_self))
     def _():
-        mask_go(0)
+        mask_go_to(c)
 
     @pl.when(mask_self)
     def _():
         maskg[mask_slot] = masks_s[c]
 
-    row_send(p0g.at[r], p0g.at[r], p0_m)
     rc(v2.at[k_core], v2.at[k_core], v_m.at[0], v_m.at[1], mate, c).start()
     row_send(p1g.at[r], p1g.at[r], p1_m)
     row_send(pcg.at[r], pcg.at[r], pc_m)
@@ -530,9 +534,6 @@
     restricted = g["scale_e1"] * restricted
     for q in range(planes):
         part_buf[q] = restricted[q * Q1:(q + 1) * Q1].astype(bf16)
-
-    near_z = z + 1 - 2 * lax.rem(z, 2)
-    far_first = (jnp.where(z < 2, 3, 0), jnp.where(z < 2, 2, 1), near_z)
 
     def z_send(src_of, dst, m):
         for q in far_first:

time: 36 us -> 35.6 us (0.989)
  Pallas kernels: 35.2 us -> 34.6 us
    pallas_call x1, Pallas kernels: 34.5 us -> 33.9 us  [fused(): pl.pallas_call(functools.partial(cycle_kernel, g), out_shape=tuple((jax.S...]
where the time goes in v7:
time: 35.6 us; the launch traced here: 35.3 us
  Pallas kernels  34.6 us (97%)
  between operations  0.64 us (2%)
    pallas_call x1, Pallas kernels, fused(): pl.pallas_call(functools.partial(cycle_kernel, g), out_shape=tuple((jax.S...  33.9 us
    pallas_call x1, Pallas kernels, fused(): pl.pallas_call(finish_kernel, grid=(1,), out_shape=tuple((jax.ShapeDtypeS...  0.72 us

profile of v7, /device:TPU:0, one launch (start us, length us, event | category | flops | bytes accessed | tf_op | source)
XLA Modules:
  0.0 35.3 jit_solution(14539716771879773882)
XLA Ops:
  0.6 33.9 %shard_map.111 = (f32[256,128]{1,0:T(8,128)S(1)}, f32[256,128]{1,0:T(8,128)S(1)}, f32[64,128]{1,0:T(8,128)S(1)}, f32[8,128]{1,0:T(8,128)S(1)}) custom-call(bf16[2048,128]{1,0:T(8,128)(2,1)} %vals_h.1, bf16[2,2048]{1,0:T(2,128)(2,1)} %points0_h.1, bf16[2,512]{1,0:T(2,128)(2,1)} %points1_h.1, bf16[2,64]{1,0:T(2,128)(2,1)} %points2_h.1, ...), custom_call_target="tpu_custom_call" | custom-call | tf_op jit(solution)/shard_map/pallas_call | solution.py:698
  34.5 0.7 %shard_map.112 = (f32[256,128]{1,0:T(8,128)}, f32[256,128]{1,0:T(8,128)}, f32[64,128]{1,0:T(8,128)}, f32[1,1]{1,0:T(1,128)}) custom-call(f32[256,128]{1,0:T(8,128)S(1)} %get-tuple-element.12.fine, f32[256,128]{1,0:T(8,128)S(1)} %get-tuple-element.13.mid, f32[64,128]{1,0:T(8,128)S(1)} %get-tuple-element.14.coarse, f32[8,128]{1,0:T(8,128)S(1)} %get-tuple-element.15.norm), custom_call_target="tpu_custom_call" | custom-call | tf_op jit(solution)/shard_map/pallas_call | solution.py:707
